TPU v7x, 32 devices: a whole 2x2x4 slice. The times are simulated.
32 devices in a mesh: row: 4 (over x, core), col: 8 (over z, y).
Axes of the slice: x: 2, y: 2, z: 4, core: 2. Of those that a mesh axis runs over, the one named last changes fastest.
Arguments:
- latent: bfloat16 [24, 96, 1536], P('row', 'col'), may hold values from -6 to 6
- attn_shift: float32 [1536], replicated, may hold values from -3 to 3
- attn_scale: float32 [1536], replicated, may hold values from -2.5 to 2.5
- attn_gate: float32 [1536], replicated, may hold values from 1 to 3
- final_shift: float32 [1536], replicated, may hold values from -3 to 3
- final_scale: float32 [1536], replicated, may hold values from -2.5 to 2.5
- q_weight: bfloat16 [1536, 768], replicated, may hold values from -2 to 2
- k_weight: bfloat16 [1536, 768], replicated, may hold values from -2 to 2
- v_weight: bfloat16 [1536, 768], replicated, may hold values from -0.15625 to 0.15625
- o_weight: bfloat16 [768, 1536], replicated, may hold values from -0.21875 to 0.21875
- out_weight: bfloat16 [1536, 64], replicated, may hold values from -0.15625 to 0.15625
- neighbour_mask: int32 [4, 8, 4], P('row', 'col'), may hold values 0 or 1
- blend_weight: float32 [32, 128], P('row', 'col'), may hold values from 0.25 to 4
Outputs:
- latent_out: float32 [24, 6144], P('row', 'col')
All inputs are finite; a program needn't handle non-finite values. No bound on the sum of `neighbour_mask` on one device may be relied on, other than what follows from the above.
Results may differ from a plain program's by a relative error of at most 0.008.
The roundings to bfloat16 on the way count: a program that leaves them out, or rounds other values in their place, can miss the bound.
Values may be sent and summed in bfloat16 or wider, within the bound.
No kernel may reach another device: no remote copies, remote signals or barrier semaphores. Data moves between devices by JAX's collectives and lax.ppermute only.
A program may use at most 64 MiB of HBM per device.

v0:
```python
import jax
import jax.numpy as jnp
from jax import lax
from jax.sharding import PartitionSpec as P

D = 1536
HD = 64
HEADS = 12
P_SIZE = 64
TH = 6
TW = 12
EH = 2
EW = 4
WH = 8
WW = 16


EPSILON = 1e-06
BLOCKED = -1e30


def from_behind(block, axis, distance):
    devices = range(lax.axis_size(axis))
    route = [((i - distance) % len(devices), i) for i in devices]
    return lax.ppermute(block, axis, route)


def layer_norm(features):
    center = features - jnp.mean(features, axis=-1, keepdims=True)
    spread = jnp.mean(center * center, axis=-1, keepdims=True)
    return center * lax.rsqrt(spread + EPSILON)


def partial_state(queries, key_rows, values):
    count_q = queries.shape[0]
    count_k = key_rows.shape[0]
    query_h = queries.reshape(count_q, HEADS, HD)
    key_h = key_rows.reshape(count_k, HEADS, HD)
    value_h = values.reshape(count_k, HEADS, HD)
    scores = (
        jnp.einsum("qhd,khd->hqk", query_h, key_h, preferred_element_type=jnp.float32) / HD**0.5
    )
    row_top = jnp.max(scores, axis=-1)
    exp_scores = jnp.exp(scores - row_top[:, :, None])
    row_mass = jnp.sum(exp_scores, axis=-1)
    output = jnp.einsum(
        "hqk,khd->qhd", exp_scores.astype(jnp.bfloat16), value_h, preferred_element_type=jnp.float32
    )
    return (row_top, row_mass, output.reshape(count_q, HEADS * HD))


def masked_state(softmax_state, live_flag):
    row_top, row_mass, output = softmax_state
    return (jnp.where(live_flag > 0, row_top, BLOCKED), row_mass * live_flag, output * live_flag)


def merge_state(earlier, second):
    row_top = jnp.maximum(earlier[0], second[0])
    scale_a = jnp.exp(earlier[0] - row_top)
    scale_b = jnp.exp(second[0] - row_top)
    row_mass = earlier[1] * scale_a + second[1] * scale_b
    row_count = earlier[2].shape[0]
    output = earlier[2].reshape(row_count, HEADS, HD) * scale_a.T[:, :, None]
    output = output + second[2].reshape(row_count, HEADS, HD) * scale_b.T[:, :, None]
    return (row_top, row_mass, output.reshape(row_count, HEADS * HD))


def shards(
    latent,
    attn_shift,
    attn_scale,
    attn_gate,
    final_shift,
    final_scale,
    q_weight,
    k_weight,
    v_weight,
    o_weight,
    out_weight,
    neighbour_mask,
    blend_weight,
):
    right_part = from_behind(latent[:, :EW], "col", -1)
    widened = jnp.concatenate([latent, right_part], axis=1)
    lower_part = from_behind(widened[:EH], "row", -1)
    window = jnp.concatenate([widened, lower_part], axis=0).reshape(WH * WW, D)
    normed = (layer_norm(window.astype(jnp.float32)) * (1.0 + attn_scale) + attn_shift).astype(
        jnp.bfloat16
    )
    queries = jnp.dot(normed, q_weight, preferred_element_type=jnp.float32).astype(jnp.bfloat16)
    key_rows = jnp.dot(normed, k_weight, preferred_element_type=jnp.float32).astype(jnp.bfloat16)
    values = jnp.dot(normed, v_weight, preferred_element_type=jnp.float32).astype(jnp.bfloat16)
    live_flags = neighbour_mask.reshape(4).astype(jnp.float32)
    softmax_state = partial_state(queries, key_rows, values)

    def from_cols(offset):
        return from_behind((key_rows, values), "col", offset)

    def from_rows(offset):
        return from_behind((key_rows, values), "row", offset)

    arrived = [from_rows(1), from_rows(-1), from_cols(1), from_cols(-1)]
    for neighbour_slot, kv_pair in enumerate(arrived):
        remote = partial_state(queries, kv_pair[0], kv_pair[1])
        softmax_state = merge_state(softmax_state, masked_state(remote, live_flags[neighbour_slot]))
    row_top, row_mass, output = softmax_state
    row_count = output.shape[0]
    attended = (
        (output.reshape(row_count, HEADS, HD) / row_mass.T[:, :, None])
        .reshape(row_count, HEADS * HD)
        .astype(jnp.bfloat16)
    )
    mixed_sum = window.astype(jnp.float32) + attn_gate * jnp.dot(
        attended, o_weight, preferred_element_type=jnp.float32
    )
    final_normed = (layer_norm(mixed_sum) * (1.0 + final_scale) + final_shift).astype(jnp.bfloat16)
    patch = jnp.dot(final_normed, out_weight, preferred_element_type=jnp.float32)
    numerator = blend_weight[:, :, None] * patch.reshape(WH, WW, P_SIZE)
    spill_over = from_behind(
        (numerator[:, TW:].reshape(WH, EW * P_SIZE), blend_weight[:, TW:]), "col", 1
    )
    num_part = numerator[:, :TW].at[:, :EW].add(spill_over[0].reshape(WH, EW, P_SIZE))
    weight_part = blend_weight[:, :TW].at[:, :EW].add(spill_over[1])
    from_above = from_behind((num_part[TH:].reshape(EH, TW * P_SIZE), weight_part[TH:]), "row", 1)
    num_top = num_part[:TH].at[:EH].add(from_above[0].reshape(EH, TW, P_SIZE))
    weight_top = weight_part[:TH].at[:EH].add(from_above[1])
    return (num_top / weight_top[:, :, None]).reshape(TH, TW * P_SIZE)


def solution(mesh):
    in_specs = (
        P("row", "col", None),
        P(),
        P(),
        P(),
        P(),
        P(),
        P(),
        P(),
        P(),
        P(),
        P(),
        P("row", "col", None),
        P("row", "col"),
    )
    out_specs = P("row", "col")
    return jax.shard_map(shards, mesh=mesh, in_specs=in_specs, out_specs=out_specs, check_vma=False)
```

profile of v0, /device:TPU:0, one launch (start us, length us, event | category | flops | bytes accessed | tf_op | source)
XLA Modules:
  0.0 92.3 jit_solution(1079459154069781894)
XLA Ops:
  1.8 6.1 %collective-permute-start = (bf16[6,4,1536]{2,1,0:T(4,128)(2,1)S(1)}, bf16[6,4,1536]{2,1,0:T(4,128)(2,1)S(1)}, u32[]{:S(2)}, u32[]{:S(2)}) collective-permute-start(bf16[6,4,1536]{2,1,0:T(4,128)(2,1)S(1)} %slice.136), channel_id=1, source_target_pairs={{1,0},{2,1},{3,2},{4,3},{5,4},{6,5},{7,6},{0,7},{9,8},{10,9},{11,1... | collective-permute-start | bytes 221192 | tf_op jit(solution)/shard_map/ppermute | solution.py:25
  20.6 2.8 %convolution_convert_fusion = bf16[128,768]{1,0:T(8,128)(2,1)} fusion(bf16[128,1536]{1,0:T(8,128)(2,1)S(1)} %fusion.22, bf16[1536,768]{1,0:T(8,128)(2,1)} %param.28), kind=kOutput, calls=%fused_computation.30 | convolution fusion | flops 302088192 | bytes 2949120 | tf_op jit(solution)/shard_map/dot_general | solution.py:91
  24.3 4.7 %collective-permute-start.8 = (bf16[128,768]{1,0:T(8,128)(2,1)}, bf16[128,768]{1,0:T(8,128)(2,1)}, u32[]{:S(2)}, u32[]{:S(2)}) collective-permute-start(bf16[128,768]{1,0:T(8,128)(2,1)} %convolution_convert_fusion), channel_id=1, source_target_pairs={{1,0},{2,1},{3,2},{4,3},{5,4},{6,5},{7,6},{0,7},{9,8},{10,9},{11,1... | collective-permute-start | bytes 589832 | tf_op jit(solution)/shard_map/ppermute | solution.py:25
  29.1 1.8 %copy.37 = bf16[128,768]{0,1:T(8,128)(2,1)} copy(bf16[128,768]{1,0:T(8,128)(2,1)} %convolution_convert_fusion) | data formatting | bytes 393216 | tf_op jit(solution)/shard_map/convert_element_type | solution.py:91
  30.8 2.1 %convolution_convert_fusion.1 = bf16[128,768]{1,0:T(8,128)(2,1)S(1)} fusion(bf16[128,1536]{1,0:T(8,128)(2,1)S(1)} %fusion.22, bf16[1536,768]{1,0:T(8,128)(2,1)} %param.27), kind=kOutput, calls=%fused_computation.31 | convolution fusion | flops 302088192 | bytes 2949120 | tf_op jit(solution)/shard_map/dot_general | solution.py:90
  33.1 2.9 %convolution_convert_fusion.2 = bf16[128,768]{1,0:T(8,128)(2,1)} fusion(bf16[128,1536]{1,0:T(8,128)(2,1)S(1)} %fusion.22, bf16[1536,768]{1,0:T(8,128)(2,1)} %param.29), kind=kOutput, calls=%fused_computation.32 | convolution fusion | flops 302088192 | bytes 2949120 | tf_op jit(solution)/shard_map/dot_general | solution.py:92
  36.0 1.7 %copy.35 = bf16[128,768]{0,1:T(8,128)(2,1)} copy(bf16[128,768]{1,0:T(8,128)(2,1)} %convolution_convert_fusion.2) | data formatting | bytes 393216 | tf_op jit(solution)/shard_map/convert_element_type | solution.py:92
  37.7 2.1 %fusion.68 = (f32[12,128]{1,0:T(8,128)S(1)}, f32[12,128,128]{1,2,0:T(8,128)}) fusion(bf16[128,12,64]{0,2,1:T(8,128)(2,1)S(1)} %bitcast.184, bf16[128,12,64]{0,2,1:T(8,128)(2,1)} %bitcast.192), kind=kOutput, calls=%fused_computation.112 | convolution fusion | flops 25557504 | bytes 1185792 | tf_op jit(solution)/shard_map/qhd,khd->hqk/dot_general | solution.py:41
  40.9 1.7 %collective-permute-start.5 = (bf16[128,768]{1,0:T(8,128)(2,1)}, bf16[128,768]{1,0:T(8,128)(2,1)}, u32[]{:S(2)}, u32[]{:S(2)}) collective-permute-start(bf16[128,768]{1,0:T(8,128)(2,1)} %convolution_convert_fusion.2), channel_id=1, source_target_pairs={{8,0},{16,8},{24,16},{0,24},{9,1},{17,9},{25,17},{1,25},{10,2},{18... | collective-permute-start | bytes 589832 | tf_op jit(solution)/shard_map/ppermute | solution.py:25
  45.2 1.8 %fusion.70 = (f32[12,128]{1,0:T(8,128)}, f32[12,128,128]{1,2,0:T(8,128)}) fusion(bf16[128,12,64]{0,2,1:T(8,128)(2,1)S(1)} %bitcast.186, bf16[128,12,64]{0,2,1:T(8,128)(2,1)S(1)} %bitcast.198), kind=kOutput, calls=%fused_computation.114 | convolution fusion | flops 25557504 | bytes 1185792 | tf_op jit(solution)/shard_map/qhd,khd->hqk/dot_general | solution.py:41
  47.0 4.7 %collective-permute-start.9 = (bf16[128,768]{1,0:T(8,128)(2,1)}, bf16[128,768]{1,0:T(8,128)(2,1)}, u32[]{:S(2)}, u32[]{:S(2)}) collective-permute-start(bf16[128,768]{1,0:T(8,128)(2,1)} %convolution_convert_fusion.2), channel_id=1, source_target_pairs={{1,0},{2,1},{3,2},{4,3},{5,4},{6,5},{7,6},{0,7},{9,8},{10,9},{11,1... | collective-permute-start | bytes 589832 | tf_op jit(solution)/shard_map/ppermute | solution.py:25
  52.8 1.8 %fusion.67 = (f32[12,128]{1,0:T(8,128)}, f32[12,128,128]{1,2,0:T(8,128)}) fusion(bf16[128,12,64]{0,2,1:T(8,128)(2,1)S(1)} %bitcast.187, bf16[128,12,64]{0,2,1:T(8,128)(2,1)S(1)} %bitcast.199), kind=kOutput, calls=%fused_computation.111 | convolution fusion | flops 25557504 | bytes 1185792 | tf_op jit(solution)/shard_map/qhd,khd->hqk/dot_general | solution.py:41
  56.1 1.7 %fusion.31 = f32[12,128]{1,0:T(8,128)S(1)} fusion(f32[12,128,128]{1,2,0:T(8,128)} %get-tuple-element.67, f32[12,128]{1,0:T(8,128)} %get-tuple-element.66), kind=kLoop, calls=%fused_computation.54 | loop fusion | flops 391680 | bytes 798720 | tf_op jit(solution)/shard_map/reduce_sum | solution.py:45
  59.1 3.3 %fusion.48 = (f32[128,12]{0,1:T(8,128)}, f32[128,12]{0,1:T(8,128)}, f32[128,12]{0,1:T(8,128)}, f32[128,12]{0,1:T(8,128)}, f32[128,12]{0,1:T(8,128)}, /*index=5*/...) fusion(f32[12,128]{1,0:T(8,128)S(1)} %get-tuple-element.78, f32[12,128]{1,0:T(8,128)S(1)} %fusion.31, ...), kind=kLoop, calls=%fused_computation.76 | loop fusion | flops 49152 | bytes 116756 | tf_op jit(solution)/shard_map/add | solution.py:61
  62.6 1.7 %copy.43 = bf16[128,768]{0,1:T(8,128)(2,1)} copy(bf16[128,768]{1,0:T(8,128)(2,1)} %collective-permute-done.5) | data formatting | bytes 393216 | tf_op jit(solution)/shard_map/ppermute | solution.py:25
  64.4 2.9 %fusion.15 = f32[128,12,64]{0,2,1:T(8,128)} fusion(bf16[128,12,64]{0,2,1:T(8,128)(2,1)} %bitcast.193, f32[12,128,128]{1,2,0:T(8,128)} %get-tuple-element.73, f32[12,128]{1,0:T(8,128)} %get-tuple-element.72, f32[128,12]{0,1:T(8,128)} %get-tuple-element.59, f32[]{:T(128)} %bitcast.11), kind=kOutput, calls=%fused_computation.26 | convolution fusion | flops 25755648 | bytes 1388548 | tf_op jit(solution)/shard_map/hqk,khd->qhd/dot_general | solution.py:46
  67.2 1.7 %copy.46 = bf16[128,768]{0,1:T(8,128)(2,1)} copy(bf16[128,768]{1,0:T(8,128)(2,1)} %collective-permute-done.7) | data formatting | bytes 393216 | tf_op jit(solution)/shard_map/ppermute | solution.py:25
  69.0 2.6 %fusion.16 = f32[128,12,64]{0,2,1:T(8,128)} fusion(bf16[128,12,64]{0,2,1:T(8,128)(2,1)} %bitcast.194, f32[12,128,128]{1,2,0:T(8,128)S(1)} %get-tuple-element.71, f32[12,128]{1,0:T(8,128)S(1)} %get-tuple-element.70, f32[128,12]{0,1:T(8,128)} %get-tuple-element.60, f32[]{:T(128)} %bitcast.16), kind=kOutput, calls=%fused_computation.27 | convolution fusion | flops 25755648 | bytes 1388548 | tf_op jit(solution)/shard_map/hqk,khd->qhd/dot_general | solution.py:46
  71.5 1.7 %copy.49 = bf16[128,768]{0,1:T(8,128)(2,1)} copy(bf16[128,768]{1,0:T(8,128)(2,1)} %collective-permute-done.9) | data formatting | bytes 393216 | tf_op jit(solution)/shard_map/ppermute | solution.py:25
  73.3 2.9 %fusion.17 = f32[128,12,64]{0,2,1:T(8,128)} fusion(bf16[128,12,64]{0,2,1:T(8,128)(2,1)} %bitcast.195, f32[12,128,128]{1,2,0:T(8,128)} %get-tuple-element.67, f32[12,128]{1,0:T(8,128)S(1)} %copy-done.8, f32[128,12]{0,1:T(8,128)} %get-tuple-element.61, f32[]{:T(128)} %bitcast.21), kind=kOutput, calls=%fused_computation.28 | convolution fusion | flops 25755648 | bytes 1388548 | tf_op jit(solution)/shard_map/hqk,khd->qhd/dot_general | solution.py:46
  76.1 1.7 %copy.40 = bf16[128,768]{0,1:T(8,128)(2,1)} copy(bf16[128,768]{1,0:T(8,128)(2,1)} %collective-permute-done.3) | data formatting | bytes 393216 | tf_op jit(solution)/shard_map/ppermute | solution.py:25
  77.9 2.5 %fusion.18 = bf16[128,12,64]{0,2,1:T(8,128)(2,1)S(1)} fusion(f32[128,12,64]{0,2,1:T(8,128)} %fusion.17, f32[128,12,64]{0,2,1:T(8,128)} %fusion.16, f32[128,12,64]{0,2,1:T(8,128)} %fusion.15, f32[128,12,64]{0,2,1:T(8,128)S(1)} %fusion.1, bf16[128,12,64]{0,2,1:T(8,128)(2,1)} %bitcast.191, f32[12,128,128]{1,2,0:T(8,128)} %copy-done.4, ...), kind=kOutput, calls=%fused_computation.29 | convolution fusion | flops 26640384 | bytes 2789380 | tf_op jit(solution)/shard_map/hqk,khd->qhd/dot_general | solution.py:46
  84.1 4.1 %collective-permute-done.10 = f32[8,256]{1,0:T(8,128)S(1)} collective-permute-done((f32[8,256]{1,0:T(8,128)S(1)}, f32[8,256]{1,0:T(8,128)S(1)}, u32[]{:S(2)}, u32[]{:S(2)}) %collective-permute-start.10) | collective-permute-done | bytes 8224 | tf_op jit(solution)/shard_map/ppermute | solution.py:25
  88.5 3.0 %collective-permute-done.11 = f32[2,768]{1,0:T(2,128)S(1)} collective-permute-done((f32[2,768]{1,0:T(2,128)S(1)}, f32[2,768]{1,0:T(2,128)S(1)}, u32[]{:S(2)}, u32[]{:S(2)}) %collective-permute-start.11) | collective-permute-done | bytes 6176 | tf_op jit(solution)/shard_map/ppermute | solution.py:25
  (106 shorter events, 25.2 us)
Async XLA Ops:
  0.0 80.4 %copy-start = (bf16[768,1536]{1,0:T(8,128)(2,1)S(1)}, bf16[768,1536]{1,0:T(8,128)(2,1)}, u32[]{:S(2)}) copy-start(bf16[768,1536]{1,0:T(8,128)(2,1)} %param.30) | copy-start | bytes 7077892
  0.8 10.3 %copy-start.11 = (f32[8,16]{1,0:T(8,128)}, f32[8,16]{1,0:T(8,128)S(1)}, u32[]{:S(2)}) copy-start(f32[8,16]{1,0:T(8,128)S(1)} %copy.63) | copy-start | bytes 1540
  1.8 9.4 %collective-permute-start = (bf16[6,4,1536]{2,1,0:T(4,128)(2,1)S(1)}, bf16[6,4,1536]{2,1,0:T(4,128)(2,1)S(1)}, u32[]{:S(2)}, u32[]{:S(2)}) collective-permute-start(bf16[6,4,1536]{2,1,0:T(4,128)(2,1)S(1)} %slice.136), channel_id=1, source_target_pairs={{1,0},{2,1},{3,2},{4,3},{5,4},{6,5},{7,6},{0,7},{9,8},{10,9},{11,1... | collective-permute-start | bytes 221192 | tf_op jit(solution)/shard_map/ppermute | solution.py:25
  8.5 73.4 %collective-permute-start.12 = (f32[8,4]{1,0:T(8,128)}, f32[8,4]{1,0:T(8,128)}, u32[]{:S(2)}, u32[]{:S(2)}) collective-permute-start(f32[8,4]{1,0:T(8,128)} %slice.150), channel_id=1, source_target_pairs={{7,0},{0,1},{1,2},{2,3},{3,4},{4,5},{5,6},{6,7},{15,8},{8,9},{9,10... | collective-permute-start | bytes 392 | tf_op jit(solution)/shard_map/ppermute | solution.py:25
  12.1 4.7 %collective-permute-start.1 = (bf16[2,16,1536]{2,1,0:T(8,128)(2,1)S(1)}, bf16[2,16,1536]{2,1,0:T(8,128)(2,1)S(1)}, u32[]{:S(2)}, u32[]{:S(2)}) collective-permute-start(bf16[2,16,1536]{2,1,0:T(8,128)(2,1)S(1)} %pad_maximum_fusion.1), channel_id=1, source_target_pairs={{8,0},{16,8},{24,16},{0,24},{9,1},{17,9},{25,17},{1,25},{10,2},{18... | collective-permute-start | bytes 294920 | tf_op jit(solution)/shard_map/ppermute | solution.py:25
  23.4 17.5 %collective-permute-start.6 = (bf16[128,768]{1,0:T(8,128)(2,1)}, bf16[128,768]{1,0:T(8,128)(2,1)}, u32[]{:S(2)}, u32[]{:S(2)}) collective-permute-start(bf16[128,768]{1,0:T(8,128)(2,1)} %convolution_convert_fusion), channel_id=1, source_target_pairs={{7,0},{0,1},{1,2},{2,3},{3,4},{4,5},{5,6},{6,7},{15,8},{8,9},{9,10... | collective-permute-start | bytes 589832 | tf_op jit(solution)/shard_map/ppermute | solution.py:25
  23.4 20.7 %collective-permute-start.4 = (bf16[128,768]{1,0:T(8,128)(2,1)}, bf16[128,768]{1,0:T(8,128)(2,1)}, u32[]{:S(2)}, u32[]{:S(2)}) collective-permute-start(bf16[128,768]{1,0:T(8,128)(2,1)} %convolution_convert_fusion), channel_id=1, source_target_pairs={{8,0},{16,8},{24,16},{0,24},{9,1},{17,9},{25,17},{1,25},{10,2},{18... | collective-permute-start | bytes 589832 | tf_op jit(solution)/shard_map/ppermute | solution.py:25
  24.3 22.7 %collective-permute-start.8 = (bf16[128,768]{1,0:T(8,128)(2,1)}, bf16[128,768]{1,0:T(8,128)(2,1)}, u32[]{:S(2)}, u32[]{:S(2)}) collective-permute-start(bf16[128,768]{1,0:T(8,128)(2,1)} %convolution_convert_fusion), channel_id=1, source_target_pairs={{1,0},{2,1},{3,2},{4,3},{5,4},{6,5},{7,6},{0,7},{9,8},{10,9},{11,1... | collective-permute-start | bytes 589832 | tf_op jit(solution)/shard_map/ppermute | solution.py:25
  29.0 25.6 %collective-permute-start.2 = (bf16[128,768]{1,0:T(8,128)(2,1)}, bf16[128,768]{1,0:T(8,128)(2,1)}, u32[]{:S(2)}, u32[]{:S(2)}) collective-permute-start(bf16[128,768]{1,0:T(8,128)(2,1)} %convolution_convert_fusion), channel_id=1, source_target_pairs={{24,0},{0,8},{8,16},{16,24},{25,1},{1,9},{9,17},{17,25},{26,2},{2,... | collective-permute-start | bytes 589832 | tf_op jit(solution)/shard_map/ppermute | solution.py:25
  33.1 6.7 %copy-start.1 = (bf16[6,12,1536]{2,1,0:T(8,128)(2,1)S(1)}, bf16[6,12,1536]{2,1,0:T(8,128)(2,1)}, u32[]{:S(2)}) copy-start(bf16[6,12,1536]{2,1,0:T(8,128)(2,1)} %param.21) | copy-start | bytes 663556
  40.9 21.8 %collective-permute-start.5 = (bf16[128,768]{1,0:T(8,128)(2,1)}, bf16[128,768]{1,0:T(8,128)(2,1)}, u32[]{:S(2)}, u32[]{:S(2)}) collective-permute-start(bf16[128,768]{1,0:T(8,128)(2,1)} %convolution_convert_fusion.2), channel_id=1, source_target_pairs={{8,0},{16,8},{24,16},{0,24},{9,1},{17,9},{25,17},{1,25},{10,2},{18... | collective-permute-start | bytes 589832 | tf_op jit(solution)/shard_map/ppermute | solution.py:25
  44.0 23.2 %collective-permute-start.7 = (bf16[128,768]{1,0:T(8,128)(2,1)}, bf16[128,768]{1,0:T(8,128)(2,1)}, u32[]{:S(2)}, u32[]{:S(2)}) collective-permute-start(bf16[128,768]{1,0:T(8,128)(2,1)} %convolution_convert_fusion.2), channel_id=1, source_target_pairs={{7,0},{0,1},{1,2},{2,3},{3,4},{4,5},{5,6},{6,7},{15,8},{8,9},{9,10... | collective-permute-start | bytes 589832 | tf_op jit(solution)/shard_map/ppermute | solution.py:25
  47.0 24.5 %collective-permute-start.9 = (bf16[128,768]{1,0:T(8,128)(2,1)}, bf16[128,768]{1,0:T(8,128)(2,1)}, u32[]{:S(2)}, u32[]{:S(2)}) collective-permute-start(bf16[128,768]{1,0:T(8,128)(2,1)} %convolution_convert_fusion.2), channel_id=1, source_target_pairs={{1,0},{2,1},{3,2},{4,3},{5,4},{6,5},{7,6},{0,7},{9,8},{10,9},{11,1... | collective-permute-start | bytes 589832 | tf_op jit(solution)/shard_map/ppermute | solution.py:25
  54.6 21.5 %collective-permute-start.3 = (bf16[128,768]{1,0:T(8,128)(2,1)}, bf16[128,768]{1,0:T(8,128)(2,1)}, u32[]{:S(2)}, u32[]{:S(2)}) collective-permute-start(bf16[128,768]{1,0:T(8,128)(2,1)} %convolution_convert_fusion.2), channel_id=1, source_target_pairs={{24,0},{0,8},{8,16},{16,24},{25,1},{1,9},{9,17},{17,25},{26,2},{2,... | collective-permute-start | bytes 589832 | tf_op jit(solution)/shard_map/ppermute | solution.py:25
  55.8 3.3 %copy-start.7 = (f32[12,128]{1,0:T(8,128)S(1)}, f32[12,128]{1,0:T(8,128)}, u32[]{:S(2)}) copy-start(f32[12,128]{1,0:T(8,128)} %get-tuple-element.66) | copy-start | bytes 18436
  56.1 6.5 %copy-start.4 = (f32[12,128,128]{1,2,0:T(8,128)}, f32[12,128,128]{1,2,0:T(8,128)S(1)}, u32[]{:S(2)}) copy-start(f32[12,128,128]{1,2,0:T(8,128)S(1)} %get-tuple-element.75) | copy-start | bytes 2359300
  56.1 6.5 %copy-start.9 = (f32[12,128]{1,0:T(8,128)}, f32[12,128]{1,0:T(8,128)S(1)}, u32[]{:S(2)}) copy-start(f32[12,128]{1,0:T(8,128)S(1)} %get-tuple-element.74) | copy-start | bytes 18436
  56.1 6.2 %copy-start.6 = (bf16[128,768]{0,1:T(8,128)(2,1)S(1)}, bf16[128,768]{0,1:T(8,128)(2,1)}, u32[]{:S(2)}) copy-start(bf16[128,768]{0,1:T(8,128)(2,1)} %copy.35) | copy-start | bytes 589828
  62.6 10.7 %copy-start.8 = (f32[12,128]{1,0:T(8,128)S(1)}, f32[12,128]{1,0:T(8,128)}, u32[]{:S(2)}) copy-start(f32[12,128]{1,0:T(8,128)} %get-tuple-element.66) | copy-start | bytes 18436
  73.2 7.2 %copy-start.5 = (f32[8,16,1536]{2,1,0:T(8,128)S(1)}, f32[8,16,1536]{2,1,0:T(8,128)}, u32[]{:S(2)}) copy-start(f32[8,16,1536]{2,1,0:T(8,128)} %fusion.59) | copy-start | bytes 2359300
  73.2 7.2 %copy-start.13 = (f32[1536]{0:T(1024)S(1)}, f32[1536]{0:T(1024)}, u32[]{:S(2)}) copy-start(f32[1536]{0:T(1024)} %param.24) | copy-start | bytes 18436
  81.9 6.3 %collective-permute-start.10 = (f32[8,256]{1,0:T(8,128)S(1)}, f32[8,256]{1,0:T(8,128)S(1)}, u32[]{:S(2)}, u32[]{:S(2)}) collective-permute-start(f32[8,256]{1,0:T(8,128)S(1)} %reshape.268), channel_id=1, source_target_pairs={{7,0},{0,1},{1,2},{2,3},{3,4},{4,5},{5,6},{6,7},{15,8},{8,9},{9,10... | collective-permute-start | bytes 24584 | tf_op jit(solution)/shard_map/ppermute | solution.py:25
  83.4 5.0 %collective-permute-start.13 = (f32[2,12]{1,0:T(2,128)S(1)}, f32[2,12]{1,0:T(2,128)S(1)}, u32[]{:S(2)}, u32[]{:S(2)}) collective-permute-start(f32[2,12]{1,0:T(2,128)S(1)} %slice.153), channel_id=1, source_target_pairs={{24,0},{0,8},{8,16},{16,24},{25,1},{1,9},{9,17},{17,25},{26,2},{2,... | collective-permute-start | bytes 296 | tf_op jit(solution)/shard_map/ppermute | solution.py:25
  88.4 3.1 %collective-permute-start.11 = (f32[2,768]{1,0:T(2,128)S(1)}, f32[2,768]{1,0:T(2,128)S(1)}, u32[]{:S(2)}, u32[]{:S(2)}) collective-permute-start(f32[2,768]{1,0:T(2,128)S(1)} %reshape.270), channel_id=1, source_target_pairs={{24,0},{0,8},{8,16},{16,24},{25,1},{1,9},{9,17},{17,25},{26,2},{2,... | collective-permute-start | bytes 18440 | tf_op jit(solution)/shard_map/ppermute | solution.py:25
  (7 other events, 12.4 us)
where the time goes:
time: 93.4 us; the launch traced here: 92.3 us
  matrix products  26.2 us (28%)
  starting transfers between devices  19.7 us (21%)
  local copies, waits for them, and re-layouts  19.6 us (21%)
  other arithmetic  16.7 us (18%)
  waiting for transfers between devices  7.14 us (8%)
  between operations  3.01 us (3%)
    ppermute x14, starting transfers between devices, from_behind(): return lax.ppermute(block, axis, route)  19.7 us
    ppermute x8, local copies, waits for them, and re-layouts, from_behind(): return lax.ppermute(block, axis, route)  11.3 us
    dot_general x5, matrix products, partial_state(): jnp.einsum('hqk,khd->qhd', exp_scores.astype(jnp.bfloat16), value_h, pref...  11 us
    ppermute x14, waiting for transfers between devices, from_behind(): return lax.ppermute(block, axis, route)  7.14 us
    dot_general x5, matrix products, partial_state(): jnp.einsum('qhd,khd->hqk', query_h, key_h, preferred_element_type=jnp.flo...  6.43 us
    add x1, other arithmetic, merge_state(): row_mass = earlier[1] * scale_a + second[1] * scale_b  3.25 us
    reduce_sum x3, other arithmetic, partial_state(): row_mass = jnp.sum(exp_scores, axis=-1)  2.88 us
    dot_general x1, matrix products, shards(): jnp.dot(normed, v_weight, preferred_element_type=jnp.float32)  2.87 us
  transfers between devices with their start and end apart: 14, of which 2 were waited for; matrix products, arithmetic and copies ran while one was open for 65% of the time, Pallas kernels for 0%

commit v1 on v0

v1 whole, which is shorter than its diff:
```python
import functools

import jax
import jax.numpy as jnp
from jax import lax
from jax.experimental import pallas as pl
from jax.experimental.pallas import tpu as pltpu
from jax.sharding import PartitionSpec as P

D = 1536
HD = 64
HEADS = 12
P_SIZE = 64
TH = 6
TW = 12
EH = 2
EW = 4
WH = 8
WW = 16
AD = HEADS * HD
PAIRS = HEADS // 2
OWN = WH * WW
SIDE = WH * TW
KEYS = OWN + 4 * SIDE
LANES = 128

EPSILON = 1e-06
BLOCKED = -1e30
F32 = jnp.float32
BF16 = jnp.bfloat16


def fetch(block, down, right):
    n_row, n_col = lax.axis_size("row"), lax.axis_size("col")
    route = [
        (((r + down) % n_row) * n_col + (c + right) % n_col, r * n_col + c)
        for r in range(n_row)
        for c in range(n_col)
    ]
    return lax.ppermute(block, ("row", "col"), route)


def layer_norm(features, scale, shift):
    center = features - jnp.mean(features, axis=-1, keepdims=True)
    spread = jnp.mean(center * center, axis=-1, keepdims=True)
    normed = center * lax.rsqrt(spread + EPSILON)
    return (normed * (1.0 + scale) + shift).astype(BF16)


def dot(a, b):
    return jnp.dot(a, b, preferred_element_type=F32)


def pack_kernel(x_ref, right_ref, lower_ref, corner_ref):
    for r in range(TH):
        right_ref[EW * r : EW * (r + 1)] = x_ref[r, :EW]
    for r in range(EH):
        lower_ref[TW * r : TW * (r + 1)] = x_ref[r]
        corner_ref[EW * r : EW * (r + 1)] = x_ref[r, :EW]


def assemble_kernel(x_ref, right_ref, lower_ref, corner_ref, win_ref, up_ref, down_ref, left_ref, out_ref):
    for r in range(WH):
        if r < TH:
            body, tail = x_ref[r], right_ref[EW * r : EW * (r + 1)]
        else:
            k = r - TH
            body, tail = lower_ref[TW * k : TW * (k + 1)], corner_ref[EW * k : EW * (k + 1)]
        row = jnp.concatenate([body, tail], axis=0)
        win_ref[WW * r : WW * (r + 1)] = row
        if r >= EH:
            up_ref[WW * (r - EH) : WW * (r - EH + 1)] = row
        if r < TH:
            down_ref[WW * r : WW * (r + 1)] = row
        left_ref[TW * r : TW * (r + 1)] = row[EW:]
        out_ref[TW * r : TW * (r + 1)] = body


def own_kernel(win_ref, scale_ref, shift_ref, qw_ref, kw_ref, vw_ref, q_ref, k_ref, v_ref):
    normed = layer_norm(win_ref[...].astype(F32), scale_ref[...], shift_ref[...])
    q_ref[...] = dot(normed, qw_ref[...]).astype(BF16)
    k_ref[...] = dot(normed, kw_ref[...]).astype(BF16)
    v_ref[...] = dot(normed, vw_ref[...]).astype(BF16)


def rest_kernel(
    mask_ref,
    win_ref,
    q_ref,
    k_ref,
    v_ref,
    up_ref,
    down_ref,
    left_ref,
    right_ref,
    scale_ref,
    shift_ref,
    gate_ref,
    fscale_ref,
    fshift_ref,
    kw_ref,
    vw_ref,
    ow_ref,
    pw_ref,
    blend_ref,
    kept_ref,
    spill_e_ref,
    spill_s_ref,
    spill_c_ref,
    normed_ref,
    keys_ref,
    vals_ref,
    att_ref,
):
    for j, side in enumerate((up_ref, down_ref, left_ref, right_ref)):
        normed_ref[SIDE * j : SIDE * (j + 1)] = layer_norm(
            side[...].astype(F32), scale_ref[...], shift_ref[...]
        )
    normed = normed_ref[...]
    keys_ref[:OWN] = k_ref[...]
    keys_ref[OWN:] = dot(normed, kw_ref[...]).astype(BF16)
    values = dot(normed, vw_ref[...]).astype(BF16)
    for p in range(PAIRS):
        vals_ref[p, :OWN, :LANES] = v_ref[:, LANES * p : LANES * (p + 1)]
        vals_ref[p, OWN:, :LANES] = values[:, LANES * p : LANES * (p + 1)]
        vals_ref[p, :, LANES:] = jnp.ones((KEYS, LANES), BF16)

    live = [mask_ref[j] for j in range(4)]
    token = lax.broadcasted_iota(jnp.int32, (1, OWN), 1)
    row, col = token // WW, token % WW
    times = (
        1
        + jnp.where(row < EH, live[0], 0)
        + jnp.where(row >= TH, live[1], 0)
        + jnp.where(col < EW, live[2], 0)
        + jnp.where(col >= TW, live[3], 0)
    ).astype(F32)
    place = lax.broadcasted_iota(jnp.int32, (1, KEYS), 1)
    shut = jnp.zeros((1, KEYS), F32)
    for j in range(4):
        inside = (place >= OWN + SIDE * j) & (place < OWN + SIDE * (j + 1))
        shut = jnp.where(inside & (live[j] == 0), BLOCKED, shut)
    times = jnp.concatenate([times, jnp.ones((1, KEYS - OWN), F32)], axis=1)
    lane = lax.broadcasted_iota(jnp.int32, (OWN, LANES), 1)
    first = lane < HD
    zero = jnp.zeros((OWN, LANES), BF16)
    for p in range(PAIRS):
        q = q_ref[:, LANES * p : LANES * (p + 1)] * BF16(HD**-0.5)
        both = jnp.concatenate([jnp.where(first, q, zero), jnp.where(first, zero, q)], axis=0)
        scores = lax.dot_general(
            both,
            keys_ref[:, LANES * p : LANES * (p + 1)],
            (((1,), (1,)), ((), ())),
            preferred_element_type=F32,
        )
        scores = scores + shut
        top = jnp.max(scores, axis=-1, keepdims=True)
        weights = (jnp.exp(scores - top) * times).astype(BF16)
        out = dot(weights, vals_ref[p])
        out = out[:, :LANES] / out[:, LANES:]
        att_ref[:, LANES * p : LANES * (p + 1)] = jnp.where(first, out[:OWN], out[OWN:]).astype(BF16)

    mixed = win_ref[...].astype(F32) + gate_ref[...] * dot(att_ref[...], ow_ref[...])
    final = layer_norm(mixed, fscale_ref[...], fshift_ref[...])
    patch = dot(final, pw_ref[...])
    spread = jnp.concatenate(
        [jnp.broadcast_to(blend_ref[r : r + 1], (WW, WW)) for r in range(WH)], axis=0
    )
    own_row = lax.broadcasted_iota(jnp.int32, (OWN, WW), 0) % WW
    own_col = lax.broadcasted_iota(jnp.int32, (OWN, WW), 1)
    b = jnp.sum(jnp.where(own_row == own_col, spread, 0.0), axis=1, keepdims=True)
    both = jnp.concatenate([b * patch, jnp.broadcast_to(b, (OWN, P_SIZE))], axis=1)
    for r in range(WH):
        at = WW * r
        if r < TH:
            kept_ref[TW * r : TW * (r + 1)] = both[at : at + TW]
            spill_e_ref[EW * r : EW * (r + 1)] = both[at + TW : at + WW]
        else:
            k = r - TH
            spill_s_ref[TW * k : TW * (k + 1)] = both[at : at + TW]
            spill_c_ref[EW * k : EW * (k + 1)] = both[at + TW : at + WW]


def blend_kernel(kept_ref, left_ref, upper_ref, corner_ref, out_ref):
    for y in range(TH):
        row = kept_ref[TW * y : TW * (y + 1)]
        head = left_ref[EW * y : EW * (y + 1)]
        if y < EH:
            row = row + upper_ref[TW * y : TW * (y + 1)]
            head = head + corner_ref[EW * y : EW * (y + 1)]
        row = jnp.concatenate([row[:EW] + head, row[EW:]], axis=0)
        ratio = row[:, :P_SIZE] / row[:, P_SIZE:]
        for x in range(TW):
            out_ref[y : y + 1, P_SIZE * x : P_SIZE * (x + 1)] = ratio[x : x + 1]


VM = pl.BlockSpec(memory_space=pltpu.VMEM)
SM = pl.BlockSpec(memory_space=pltpu.SMEM)


def call(kernel, outs, scratch=(), smem=0, limit=None):
    def run(*args):
        return pl.pallas_call(
            kernel,
            out_shape=[jax.ShapeDtypeStruct(s, d) for s, d in outs],
            in_specs=[SM] * smem + [VM] * (len(args) - smem),
            out_specs=[VM] * len(outs),
            scratch_shapes=[pltpu.VMEM(s, d) for s, d in scratch],
            compiler_params=pltpu.CompilerParams(vmem_limit_bytes=limit),
        )(*args)

    return run


MB = 1 << 20


def shards(
    latent,
    attn_shift,
    attn_scale,
    attn_gate,
    final_shift,
    final_scale,
    q_weight,
    k_weight,
    v_weight,
    o_weight,
    out_weight,
    neighbour_mask,
    blend_weight,
):
    shift, scale, gate = (v.reshape(1, D) for v in (attn_shift, attn_scale, attn_gate))
    fshift, fscale = (v.reshape(1, D) for v in (final_shift, final_scale))
    mask = neighbour_mask.reshape(4)
    halo = call(
        pack_kernel,
        [((TH * EW, D), BF16), ((EH * TW, D), BF16), ((EH * EW, D), BF16)],
        limit=4 * MB,
    )(latent)
    right, lower, corner = fetch(halo[0], 0, 1), fetch(halo[1], 1, 0), fetch(halo[2], 1, 1)
    win, to_up, to_down, to_left, to_right = call(
        assemble_kernel, [((OWN, D), BF16)] + [((SIDE, D), BF16)] * 4, limit=8 * MB
    )(latent, right, lower, corner)
    from_left, from_right = fetch(to_right, 0, -1), fetch(to_left, 0, 1)
    from_up, from_down = fetch(to_down, -1, 0), fetch(to_up, 1, 0)
    q, k, v = call(own_kernel, [((OWN, AD), BF16)] * 3, limit=24 * MB)(
        win, scale, shift, q_weight, k_weight, v_weight
    )
    kept, spill_e, spill_s, spill_c = call(
        rest_kernel,
        [
            ((TH * TW, LANES), F32),
            ((TH * EW, LANES), F32),
            ((EH * TW, LANES), F32),
            ((EH * EW, LANES), F32),
        ],
        scratch=[
            ((KEYS - OWN, D), BF16),
            ((KEYS, AD), BF16),
            ((PAIRS, KEYS, 2 * LANES), BF16),
            ((OWN, AD), BF16),
        ],
        smem=1,
        limit=32 * MB,
    )(
        mask, win, q, k, v, from_up, from_down, from_left, from_right,
        scale, shift, gate, fscale, fshift, k_weight, v_weight, o_weight, out_weight, blend_weight,
    )
    left, upper, diag = fetch(spill_e, 0, -1), fetch(spill_s, -1, 0), fetch(spill_c, -1, -1)
    (out,) = call(blend_kernel, [((TH, TW * P_SIZE), F32)], limit=4 * MB)(kept, left, upper, diag)
    return out


def solution(mesh):
    in_specs = (
        P("row", "col", None),
        P(),
        P(),
        P(),
        P(),
        P(),
        P(),
        P(),
        P(),
        P(),
        P(),
        P("row", "col", None),
        P("row", "col"),
    )
    out_specs = P("row", "col")
    return jax.shard_map(shards, mesh=mesh, in_specs=in_specs, out_specs=out_specs, check_vma=False)
```

time: 93.4 us -> 45.4 us (0.49)
  matrix products: 26.2 us -> 0 us
  other arithmetic: 16.7 us -> 0 us
  Pallas kernels: 0 us -> 7.54 us
  local copies, waits for them, and re-layouts: 19.6 us -> 13.3 us
  starting transfers between devices: 19.7 us -> 14.5 us
  between operations: 3.01 us -> 0.13 us
  waiting for transfers between devices: 7.14 us -> 9.43 us
    dot_general x15 -> x0, matrix products: 26.2 us -> none  [the longest x5 11 us: partial_state(): jnp.einsum('hqk,khd->qhd', exp_scores.astype(jnp.bfloat16), value_h, pref...]
    ppermute x8 -> x0, local copies, waits for them, and re-layouts: 11.3 us -> none  [from_behind(): return lax.ppermute(block, axis, route)]
    unnamed x37 -> x21, local copies, waits for them, and re-layouts: 0.98 us -> 9.76 us
    pallas_call x0 -> x5, Pallas kernels: none -> 7.54 us  [run(): pl.pallas_call(kernel, out_shape=[jax.ShapeDtypeStruct(s, d) for s, d in...]
    reduce_sum x6 -> x0, other arithmetic: 5.47 us -> none  [the longest x3 2.88 us: partial_state(): row_mass = jnp.sum(exp_scores, axis=-1)]
    add x3 -> x0, other arithmetic: 5.25 us -> none  [the longest x1 3.25 us: merge_state(): row_mass = earlier[1] * scale_a + second[1] * scale_b]
    ppermute x14 -> x10, starting transfers between devices: 19.7 us -> 14.5 us  [fetch(): return lax.ppermute(block, ('row', 'col'), route)]
    convert_element_type x3 -> x0, local copies, waits for them, and re-layouts: 3.66 us -> none  [the longest x1 1.76 us: shards(): jnp.dot(normed, k_weight, preferred_element_type=jnp.float32)]
  transfers between devices with their start and end apart: 14 -> 10, of which waited for: 2 -> 2; matrix products, arithmetic and copies ran while one was open for 65% -> 10% of each run, Pallas kernels for 0% -> 3%
where the time goes in v1:
time: 45.4 us; the launch traced here: 44.9 us
  starting transfers between devices  14.5 us (32%)
  local copies, waits for them, and re-layouts  13.3 us (29%)
  waiting for transfers between devices  9.43 us (21%)
  Pallas kernels  7.54 us (17%)
    ppermute x10, starting transfers between devices, fetch(): return lax.ppermute(block, ('row', 'col'), route)  14.5 us
    unnamed x21, local copies, waits for them, and re-layouts  9.76 us
    ppermute x10, waiting for transfers between devices, fetch(): return lax.ppermute(block, ('row', 'col'), route)  9.43 us
    pallas_call x5, Pallas kernels, run(): pl.pallas_call(kernel, out_shape=[jax.ShapeDtypeStruct(s, d) for s, d in...  7.54 us
    reshape x3, local copies, waits for them, and re-layouts, shards(): v.reshape(1, D)  2.1 us
    reshape x2, local copies, waits for them, and re-layouts, shards(): fshift, fscale = (v.reshape(1, D) for v in (final_shift, final_scale))  1.4 us
  transfers between devices with their start and end apart: 10, of which 2 were waited for; matrix products, arithmetic and copies ran while one was open for 10% of the time, Pallas kernels for 3%

profile of v1, /device:TPU:0, one launch (start us, length us, event | category | flops | bytes accessed | tf_op | source)
XLA Modules:
  0.0 44.9 jit_solution(944212049307706735)
XLA Ops:
  0.0 1.0 %copy-done.6 = bf16[6,12,1536]{2,1,0:T(8,128)(2,1)S(1)} copy-done((bf16[6,12,1536]{2,1,0:T(8,128)(2,1)S(1)}, bf16[6,12,1536]{2,1,0:T(8,128)(2,1)}, u32[]{:S(2)}) %copy-start.6) | copy-done | bytes 221208
  1.0 6.1 %collective-permute-start = (bf16[24,1536]{1,0:T(8,128)(2,1)S(1)}, bf16[24,1536]{1,0:T(8,128)(2,1)S(1)}, u32[]{:S(2)}, u32[]{:S(2)}) collective-permute-start(bf16[24,1536]{1,0:T(8,128)(2,1)S(1)} %get-tuple-element.20), channel_id=1, source_target_pairs={{1,0},{2,1},{3,2},{4,3},{5,4},{6,5},{7,6},{0,7},{9,8},{10,9},{11,1... | collective-permute-start | bytes 221192 | tf_op jit(solution)/shard_map/ppermute | solution.py:40
  7.1 0.7 %collective-permute-start.1 = (bf16[24,1536]{1,0:T(8,128)(2,1)S(1)}, bf16[24,1536]{1,0:T(8,128)(2,1)S(1)}, u32[]{:S(2)}, u32[]{:S(2)}) collective-permute-start(bf16[24,1536]{1,0:T(8,128)(2,1)S(1)} %get-tuple-element.21), channel_id=1, source_target_pairs={{8,0},{9,1},{10,2},{11,3},{12,4},{13,5},{14,6},{15,7},{16,8},{17,9... | collective-permute-start | bytes 221192 | tf_op jit(solution)/shard_map/ppermute | solution.py:40
  7.7 0.9 %collective-permute-start.2 = (bf16[8,1536]{1,0:T(8,128)(2,1)S(1)}, bf16[8,1536]{1,0:T(8,128)(2,1)S(1)}, u32[]{:S(2)}, u32[]{:S(2)}) collective-permute-start(bf16[8,1536]{1,0:T(8,128)(2,1)S(1)} %get-tuple-element.22), channel_id=1, source_target_pairs={{9,0},{10,1},{11,2},{12,3},{13,4},{14,5},{15,6},{8,7},{17,8},{18,9... | collective-permute-start | bytes 73736 | tf_op jit(solution)/shard_map/ppermute | solution.py:40
  8.6 2.4 %collective-permute-done.2.corner_ref = bf16[8,1536]{1,0:T(8,128)(2,1)S(1)} collective-permute-done((bf16[8,1536]{1,0:T(8,128)(2,1)S(1)}, bf16[8,1536]{1,0:T(8,128)(2,1)S(1)}, u32[]{:S(2)}, u32[]{:S(2)}) %collective-permute-start.2) | collective-permute-done | bytes 24608 | tf_op jit(solution)/shard_map/ppermute | solution.py:40
  11.0 1.0 %copy-done.7 = bf16[6,12,1536]{2,1,0:T(8,128)(2,1)S(1)} copy-done((bf16[6,12,1536]{2,1,0:T(8,128)(2,1)S(1)}, bf16[6,12,1536]{2,1,0:T(8,128)(2,1)}, u32[]{:S(2)}) %copy-start.7) | copy-done | bytes 221208
  12.1 0.8 %collective-permute-start.3 = (bf16[96,1536]{1,0:T(8,128)(2,1)S(1)}, bf16[96,1536]{1,0:T(8,128)(2,1)S(1)}, u32[]{:S(2)}, u32[]{:S(2)}) collective-permute-start(bf16[96,1536]{1,0:T(8,128)(2,1)S(1)} %get-tuple-element.27), channel_id=1, source_target_pairs={{24,0},{25,1},{26,2},{27,3},{28,4},{29,5},{30,6},{31,7},{0,8},{1,9... | collective-permute-start | bytes 884744 | tf_op jit(solution)/shard_map/ppermute | solution.py:40
  12.9 1.2 %collective-permute-start.4 = (bf16[96,1536]{1,0:T(8,128)(2,1)S(1)}, bf16[96,1536]{1,0:T(8,128)(2,1)S(1)}, u32[]{:S(2)}, u32[]{:S(2)}) collective-permute-start(bf16[96,1536]{1,0:T(8,128)(2,1)S(1)} %get-tuple-element.28), channel_id=1, source_target_pairs={{8,0},{9,1},{10,2},{11,3},{12,4},{13,5},{14,6},{15,7},{16,8},{17,9... | collective-permute-start | bytes 884744 | tf_op jit(solution)/shard_map/ppermute | solution.py:40
  14.6 4.2 %collective-permute-start.6 = (bf16[96,1536]{1,0:T(8,128)(2,1)S(1)}, bf16[96,1536]{1,0:T(8,128)(2,1)S(1)}, u32[]{:S(2)}, u32[]{:S(2)}) collective-permute-start(bf16[96,1536]{1,0:T(8,128)(2,1)S(1)} %get-tuple-element.30), channel_id=1, source_target_pairs={{1,0},{2,1},{3,2},{4,3},{5,4},{6,5},{7,6},{0,7},{9,8},{10,9},{11,1... | collective-permute-start | bytes 884744 | tf_op jit(solution)/shard_map/ppermute | solution.py:40
  18.8 0.7 %reshape.20.shift_ref = f32[1,1536]{1,0:T(1,128)S(1)} reshape(f32[1536]{0:T(1024)} %param.14) | data formatting | bytes 12288 | tf_op jit(solution)/shard_map/reshape | solution.py:233
  19.5 0.7 %reshape.19.scale_ref = f32[1,1536]{1,0:T(1,128)S(1)} reshape(f32[1536]{0:T(1024)} %param.15) | data formatting | bytes 12288 | tf_op jit(solution)/shard_map/reshape | solution.py:233
  20.2 0.7 %reshape.21.gate_ref = f32[1,1536]{1,0:T(1,128)S(1)} reshape(f32[1536]{0:T(1024)} %param.16) | data formatting | bytes 12288 | tf_op jit(solution)/shard_map/reshape | solution.py:233
  20.9 0.7 %reshape.23.fshift_ref = f32[1,1536]{1,0:T(1,128)S(1)} reshape(f32[1536]{0:T(1024)} %param.17) | data formatting | bytes 12288 | tf_op jit(solution)/shard_map/reshape | solution.py:234
  21.6 0.7 %reshape.22.fscale_ref = f32[1,1536]{1,0:T(1,128)S(1)} reshape(f32[1536]{0:T(1024)} %param.18) | data formatting | bytes 12288 | tf_op jit(solution)/shard_map/reshape | solution.py:234
  22.3 1.1 %copy.14.pw_ref = bf16[1536,64]{1,0:T(8,128)(2,1)S(1)} copy(bf16[1536,64]{0,1:T(8,128)(2,1)} %param.23) | data formatting | bytes 393216 | tf_op args[10]
  23.4 1.7 %copy-done = bf16[1536,768]{1,0:T(8,128)(2,1)S(1)} copy-done((bf16[1536,768]{1,0:T(8,128)(2,1)S(1)}, bf16[1536,768]{1,0:T(8,128)(2,1)}, u32[]{:S(2)}) %copy-start) | copy-done | bytes 2359320
  25.1 1.7 %copy-done.2 = bf16[1536,768]{1,0:T(8,128)(2,1)S(1)} copy-done((bf16[1536,768]{1,0:T(8,128)(2,1)S(1)}, bf16[1536,768]{1,0:T(8,128)(2,1)}, u32[]{:S(2)}) %copy-start.2) | copy-done | bytes 2359320
  26.8 1.7 %copy-done.4 = bf16[1536,768]{1,0:T(8,128)(2,1)S(1)} copy-done((bf16[1536,768]{1,0:T(8,128)(2,1)S(1)}, bf16[1536,768]{1,0:T(8,128)(2,1)}, u32[]{:S(2)}) %copy-start.4) | copy-done | bytes 2359320
  28.5 1.3 %shard_map.129 = (bf16[128,768]{1,0:T(8,128)(2,1)S(1)}, bf16[128,768]{1,0:T(8,128)(2,1)S(1)}, bf16[128,768]{1,0:T(8,128)(2,1)S(1)}) custom-call(bf16[128,1536]{1,0:T(8,128)(2,1)S(1)} %get-tuple-element.23.win_ref, f32[1,1536]{1,0:T(1,128)S(1)} %reshape.19.scale_ref, f32[1,1536]{1,0:T(1,128)S(1)} %reshape.20.shift_ref, bf16[1536,768]{1,0:T(8,128)(2,1)S(1)} %copy-done.4, ...), custom_call_target="tpu_custom_call" | custom-call | tf_op jit(solution)/shard_map/pallas_call | solution.py:203
  30.1 0.7 %copy-done.3 = bf16[1536,768]{1,0:T(8,128)(2,1)S(1)} copy-done((bf16[1536,768]{1,0:T(8,128)(2,1)S(1)}, bf16[1536,768]{1,0:T(8,128)(2,1)}, u32[]{:S(2)}) %copy-start.3) | copy-done | bytes 2359320
  30.8 0.7 %copy-done.5 = bf16[768,1536]{1,0:T(8,128)(2,1)S(1)} copy-done((bf16[768,1536]{1,0:T(8,128)(2,1)S(1)}, bf16[768,1536]{1,0:T(8,128)(2,1)}, u32[]{:S(2)}) %copy-start.5) | copy-done | bytes 2359320
  31.5 5.3 %shard_map.130 = (f32[72,128]{1,0:T(8,128)S(1)}, f32[24,128]{1,0:T(8,128)S(1)}, f32[24,128]{1,0:T(8,128)S(1)}, f32[8,128]{1,0:T(8,128)S(1)}) custom-call(s32[4]{0:T(128)S(1)} %bitcast.1, bf16[128,1536]{1,0:T(8,128)(2,1)S(1)} %get-tuple-element.23.win_ref, bf16[128,768]{1,0:T(8,128)(2,1)S(1)} %get-tuple-element.24.q_ref, ...), custom_call_target="tpu_custom_call" | custom-call | tf_op jit(solution)/shard_map/pallas_call | solution.py:203
  37.0 7.1 %collective-permute-done.9.corner_ref = f32[8,128]{1,0:T(8,128)S(1)} collective-permute-done((f32[8,128]{1,0:T(8,128)S(1)}, f32[8,128]{1,0:T(8,128)S(1)}, u32[]{:S(2)}, u32[]{:S(2)}) %collective-permute-start.9) | collective-permute-done | bytes 4128 | tf_op jit(solution)/shard_map/ppermute | solution.py:40
  44.1 0.8 %shard_map.131 = f32[6,768]{1,0:T(8,128)} custom-call(f32[72,128]{1,0:T(8,128)S(1)} %get-tuple-element.31.kept_ref, f32[24,128]{1,0:T(8,128)S(1)} %collective-permute-done.7.left_ref, f32[24,128]{1,0:T(8,128)S(1)} %collective-permute-done.8.upper_ref, f32[8,128]{1,0:T(8,128)S(1)} %collective-permute-done.9.corner_ref), custom_call_target="tpu_custom_call" | custom-call | tf_op jit(solution)/shard_map/pallas_call | solution.py:203
  (27 shorter events, 1.1 us)
Async XLA Ops:
  0.0 1.0 %copy-start.6 = (bf16[6,12,1536]{2,1,0:T(8,128)(2,1)S(1)}, bf16[6,12,1536]{2,1,0:T(8,128)(2,1)}, u32[]{:S(2)}) copy-start(bf16[6,12,1536]{2,1,0:T(8,128)(2,1)} %x_ref.3) | copy-start | bytes 663556
  1.0 10.0 %collective-permute-start = (bf16[24,1536]{1,0:T(8,128)(2,1)S(1)}, bf16[24,1536]{1,0:T(8,128)(2,1)S(1)}, u32[]{:S(2)}, u32[]{:S(2)}) collective-permute-start(bf16[24,1536]{1,0:T(8,128)(2,1)S(1)} %get-tuple-element.20), channel_id=1, source_target_pairs={{1,0},{2,1},{3,2},{4,3},{5,4},{6,5},{7,6},{0,7},{9,8},{10,9},{11,1... | collective-permute-start | bytes 221192 | tf_op jit(solution)/shard_map/ppermute | solution.py:40
  7.1 3.9 %collective-permute-start.1 = (bf16[24,1536]{1,0:T(8,128)(2,1)S(1)}, bf16[24,1536]{1,0:T(8,128)(2,1)S(1)}, u32[]{:S(2)}, u32[]{:S(2)}) collective-permute-start(bf16[24,1536]{1,0:T(8,128)(2,1)S(1)} %get-tuple-element.21), channel_id=1, source_target_pairs={{8,0},{9,1},{10,2},{11,3},{12,4},{13,5},{14,6},{15,7},{16,8},{17,9... | collective-permute-start | bytes 221192 | tf_op jit(solution)/shard_map/ppermute | solution.py:40
  7.7 3.3 %collective-permute-start.2 = (bf16[8,1536]{1,0:T(8,128)(2,1)S(1)}, bf16[8,1536]{1,0:T(8,128)(2,1)S(1)}, u32[]{:S(2)}, u32[]{:S(2)}) collective-permute-start(bf16[8,1536]{1,0:T(8,128)(2,1)S(1)} %get-tuple-element.22), channel_id=1, source_target_pairs={{9,0},{10,1},{11,2},{12,3},{13,4},{14,5},{15,6},{8,7},{17,8},{18,9... | collective-permute-start | bytes 73736 | tf_op jit(solution)/shard_map/ppermute | solution.py:40
  11.0 1.0 %copy-start.7 = (bf16[6,12,1536]{2,1,0:T(8,128)(2,1)S(1)}, bf16[6,12,1536]{2,1,0:T(8,128)(2,1)}, u32[]{:S(2)}) copy-start(bf16[6,12,1536]{2,1,0:T(8,128)(2,1)} %x_ref.3) | copy-start | bytes 663556
  12.1 17.7 %collective-permute-start.3 = (bf16[96,1536]{1,0:T(8,128)(2,1)S(1)}, bf16[96,1536]{1,0:T(8,128)(2,1)S(1)}, u32[]{:S(2)}, u32[]{:S(2)}) collective-permute-start(bf16[96,1536]{1,0:T(8,128)(2,1)S(1)} %get-tuple-element.27), channel_id=1, source_target_pairs={{24,0},{25,1},{26,2},{27,3},{28,4},{29,5},{30,6},{31,7},{0,8},{1,9... | collective-permute-start | bytes 884744 | tf_op jit(solution)/shard_map/ppermute | solution.py:40
  12.9 16.9 %collective-permute-start.4 = (bf16[96,1536]{1,0:T(8,128)(2,1)S(1)}, bf16[96,1536]{1,0:T(8,128)(2,1)S(1)}, u32[]{:S(2)}, u32[]{:S(2)}) collective-permute-start(bf16[96,1536]{1,0:T(8,128)(2,1)S(1)} %get-tuple-element.28), channel_id=1, source_target_pairs={{8,0},{9,1},{10,2},{11,3},{12,4},{13,5},{14,6},{15,7},{16,8},{17,9... | collective-permute-start | bytes 884744 | tf_op jit(solution)/shard_map/ppermute | solution.py:40
  14.0 15.8 %collective-permute-start.5 = (bf16[96,1536]{1,0:T(8,128)(2,1)S(1)}, bf16[96,1536]{1,0:T(8,128)(2,1)S(1)}, u32[]{:S(2)}, u32[]{:S(2)}) collective-permute-start(bf16[96,1536]{1,0:T(8,128)(2,1)S(1)} %get-tuple-element.29), channel_id=1, source_target_pairs={{7,0},{0,1},{1,2},{2,3},{3,4},{4,5},{5,6},{6,7},{15,8},{8,9},{9,10... | collective-permute-start | bytes 884744 | tf_op jit(solution)/shard_map/ppermute | solution.py:40
  14.6 15.3 %collective-permute-start.6 = (bf16[96,1536]{1,0:T(8,128)(2,1)S(1)}, bf16[96,1536]{1,0:T(8,128)(2,1)S(1)}, u32[]{:S(2)}, u32[]{:S(2)}) collective-permute-start(bf16[96,1536]{1,0:T(8,128)(2,1)S(1)} %get-tuple-element.30), channel_id=1, source_target_pairs={{1,0},{2,1},{3,2},{4,3},{5,4},{6,5},{7,6},{0,7},{9,8},{10,9},{11,1... | collective-permute-start | bytes 884744 | tf_op jit(solution)/shard_map/ppermute | solution.py:40
  23.4 1.7 %copy-start = (bf16[1536,768]{1,0:T(8,128)(2,1)S(1)}, bf16[1536,768]{1,0:T(8,128)(2,1)}, u32[]{:S(2)}) copy-start(bf16[1536,768]{1,0:T(8,128)(2,1)} %kw_ref.3) | copy-start | bytes 7077892
  25.1 1.7 %copy-start.2 = (bf16[1536,768]{1,0:T(8,128)(2,1)S(1)}, bf16[1536,768]{1,0:T(8,128)(2,1)}, u32[]{:S(2)}) copy-start(bf16[1536,768]{1,0:T(8,128)(2,1)} %vw_ref.3) | copy-start | bytes 7077892
  26.8 1.7 %copy-start.4 = (bf16[1536,768]{1,0:T(8,128)(2,1)S(1)}, bf16[1536,768]{1,0:T(8,128)(2,1)}, u32[]{:S(2)}) copy-start(bf16[1536,768]{1,0:T(8,128)(2,1)} %qw_ref.1) | copy-start | bytes 7077892
  28.4 1.7 %copy-start.1 = (bf16[1536,768]{1,0:T(8,128)(2,1)S(1)}, bf16[1536,768]{1,0:T(8,128)(2,1)}, u32[]{:S(2)}) copy-start(bf16[1536,768]{1,0:T(8,128)(2,1)} %kw_ref.3) | copy-start | bytes 7077892
  28.4 2.4 %copy-start.3 = (bf16[1536,768]{1,0:T(8,128)(2,1)S(1)}, bf16[1536,768]{1,0:T(8,128)(2,1)}, u32[]{:S(2)}) copy-start(bf16[1536,768]{1,0:T(8,128)(2,1)} %vw_ref.3) | copy-start | bytes 7077892
  28.4 3.1 %copy-start.5 = (bf16[768,1536]{1,0:T(8,128)(2,1)S(1)}, bf16[768,1536]{1,0:T(8,128)(2,1)}, u32[]{:S(2)}) copy-start(bf16[768,1536]{1,0:T(8,128)(2,1)} %ow_ref.1) | copy-start | bytes 7077892
  28.4 3.1 %copy-start.8 = (f32[8,16]{1,0:T(8,128)S(1)}, f32[8,16]{1,0:T(8,128)}, u32[]{:S(2)}) copy-start(f32[8,16]{1,0:T(8,128)} %blend_ref.1) | copy-start | bytes 1540
  28.4 3.1 %copy-start.9 = (s32[1,1,4]{2,1,0:T(1,128)S(1)}, s32[1,1,4]{2,1,0:T(1,128)}, u32[]{:S(2)}) copy-start(s32[1,1,4]{2,1,0:T(1,128)} %param.24) | copy-start | bytes 52
  36.8 7.3 %collective-permute-start.7 = (f32[24,128]{1,0:T(8,128)S(1)}, f32[24,128]{1,0:T(8,128)S(1)}, u32[]{:S(2)}, u32[]{:S(2)}) collective-permute-start(f32[24,128]{1,0:T(8,128)S(1)} %get-tuple-element.32), channel_id=1, source_target_pairs={{7,0},{0,1},{1,2},{2,3},{3,4},{4,5},{5,6},{6,7},{15,8},{8,9},{9,10... | collective-permute-start | bytes 36872 | tf_op jit(solution)/shard_map/ppermute | solution.py:40
  36.9 7.2 %collective-permute-start.8 = (f32[24,128]{1,0:T(8,128)S(1)}, f32[24,128]{1,0:T(8,128)S(1)}, u32[]{:S(2)}, u32[]{:S(2)}) collective-permute-start(f32[24,128]{1,0:T(8,128)S(1)} %get-tuple-element.33), channel_id=1, source_target_pairs={{24,0},{25,1},{26,2},{27,3},{28,4},{29,5},{30,6},{31,7},{0,8},{1,9... | collective-permute-start | bytes 36872 | tf_op jit(solution)/shard_map/ppermute | solution.py:40
  36.9 7.1 %collective-permute-start.9 = (f32[8,128]{1,0:T(8,128)S(1)}, f32[8,128]{1,0:T(8,128)S(1)}, u32[]{:S(2)}, u32[]{:S(2)}) collective-permute-start(f32[8,128]{1,0:T(8,128)S(1)} %get-tuple-element.34), channel_id=1, source_target_pairs={{31,0},{24,1},{25,2},{26,3},{27,4},{28,5},{29,6},{30,7},{7,8},{0,9... | collective-permute-start | bytes 12296 | tf_op jit(solution)/shard_map/ppermute | solution.py:40

commit v2 on v1

v2 whole, which is shorter than its diff:
```python
import jax
import jax.numpy as jnp
from jax import lax
from jax.experimental import pallas as pl
from jax.experimental.pallas import tpu as pltpu
from jax.sharding import PartitionSpec as P


D = 1536
HD = 64
HEADS = 12
P_SIZE = 64
TH = 6
TW = 12
EH = 2
EW = 4
WH = 8
WW = 16
AD = HEADS * HD
PAIRS = HEADS // 2
OWN = WH * WW
SIDE = TH * WW
MID = TW - EW
EARLY = 4 * 128
LATE = 128
PARTS = 4
LANES = 128

EPSILON = 1e-06
BLOCKED = -1e30
F32 = jnp.float32
BF16 = jnp.bfloat16


def fetch(block, down, right):
    n_row, n_col = lax.axis_size("row"), lax.axis_size("col")
    route = [
        (((r + down) % n_row) * n_col + (c + right) % n_col, r * n_col + c)
        for r in range(n_row)
        for c in range(n_col)
    ]
    return lax.ppermute(block, ("row", "col"), route)


def layer_norm(features, scale, shift):
    center = features - jnp.mean(features, axis=-1, keepdims=True)
    spread = jnp.mean(center * center, axis=-1, keepdims=True)
    normed = center * lax.rsqrt(spread + EPSILON)
    return (normed * (1.0 + scale) + shift).astype(BF16)


def dot(a, b):
    return jnp.dot(a, b, preferred_element_type=F32)


def pack_kernel(x_ref, right_ref, lower_ref, corner_ref, tile_ref, mid_ref):
    for r in range(TH):
        row = x_ref[r]
        right_ref[EW * r : EW * (r + 1)] = row[:EW]
        tile_ref[TW * r : TW * (r + 1)] = row
        mid_ref[MID * r : MID * (r + 1)] = row[EW:]
        if r < EH:
            lower_ref[TW * r : TW * (r + 1)] = row
            corner_ref[EW * r : EW * (r + 1)] = row[:EW]


def load_kernel(*refs):
    count = len(refs) - 1
    sources, targets, sems = refs[: count // 2], refs[count // 2 : count], refs[count]
    copies = []
    for i, (source, target) in enumerate(zip(sources, targets)):
        rows = source.shape[0] // PARTS
        for k in range(PARTS):
            at = pl.ds(rows * k, rows)
            copies.append(pltpu.make_async_copy(source.at[at], target.at[at], sems.at[i, k]))
    for copy in copies:
        copy.start()
    for copy in copies:
        copy.wait()


def assemble_kernel(tile_ref, right_ref, lower_ref, corner_ref, win_ref, up_ref, down_ref, late_ref):
    for r in range(WH):
        k = r - TH
        if r < TH:
            body, tail = tile_ref[TW * r : TW * (r + 1)], right_ref[EW * r : EW * (r + 1)]
        else:
            body, tail = lower_ref[TW * k : TW * (k + 1)], corner_ref[EW * k : EW * (k + 1)]
            late_ref[EW * WH + MID * k : EW * WH + MID * (k + 1)] = body[EW:]
        late_ref[EW * r : EW * (r + 1)] = tail
        row = jnp.concatenate([body, tail], axis=0)
        win_ref[WW * r : WW * (r + 1)] = row
        if r >= EH:
            up_ref[WW * (r - EH) : WW * (r - EH + 1)] = row
        if r < TH:
            down_ref[WW * r : WW * (r + 1)] = row


def own_kernel(win_ref, scale_ref, shift_ref, qw_ref, kw_ref, vw_ref, q_ref, k_ref, v_ref):
    normed = layer_norm(win_ref[...].astype(F32), vec(scale_ref), vec(shift_ref))
    q_ref[...] = (dot(normed, qw_ref[...]).astype(BF16)) * BF16(HD**-0.5)
    k_ref[...] = dot(normed, kw_ref[...]).astype(BF16)
    v_ref[...] = dot(normed, vw_ref[...]).astype(BF16)


def vec(ref):
    return ref[...].reshape(1, D)


def two_heads(q_ref, p):
    lane = lax.broadcasted_iota(jnp.int32, (OWN, LANES), 1)
    q = q_ref[:, LANES * p : LANES * (p + 1)]
    zero = jnp.zeros_like(q)
    return jnp.concatenate([jnp.where(lane < HD, q, zero), jnp.where(lane < HD, zero, q)], axis=0)


def scores_of(q, keys):
    return lax.dot_general(q, keys, (((1,), (1,)), ((), ())), preferred_element_type=F32)


def shut_row(count, spans):
    place = lax.broadcasted_iota(jnp.int32, (1, count), 1)
    shut = jnp.full((1, count), BLOCKED, F32)
    for start, stop, live in spans:
        inside = (place >= start) & (place < stop) & (live > 0)
        shut = jnp.where(inside, 0.0, shut)
    return shut


def mid_kernel(
    mask_ref, q_ref, k_ref, v_ref, up_ref, down_ref, left_ref, right_ref,
    scale_ref, shift_ref, kw_ref, vw_ref,
    state_ref, top_ref,
    normed_ref, keys_ref, vals_ref,
):
    scale, shift = vec(scale_ref), vec(shift_ref)
    spans, at = [], 0
    for j, side in enumerate((up_ref, down_ref, left_ref, right_ref)):
        size = side.shape[0]
        normed_ref[at : at + size] = layer_norm(side[...].astype(F32), scale, shift)
        spans.append((OWN + at, OWN + at + size, mask_ref[j]))
        at += size
    normed_ref[at:] = jnp.zeros((EARLY - OWN - at, D), BF16)
    normed = normed_ref[...]
    keys_ref[:OWN] = k_ref[...]
    keys_ref[OWN:] = dot(normed, kw_ref[...]).astype(BF16)
    values = dot(normed, vw_ref[...]).astype(BF16)
    for p in range(PAIRS):
        vals_ref[p, :OWN, :LANES] = v_ref[:, LANES * p : LANES * (p + 1)]
        vals_ref[p, OWN:, :LANES] = values[:, LANES * p : LANES * (p + 1)]
        vals_ref[p, :, LANES:] = jnp.ones((EARLY, LANES), BF16)
    token = lax.broadcasted_iota(jnp.int32, (1, OWN), 1)
    row, col = token // WW, token % WW
    times = 1 + jnp.where(row < EH, mask_ref[0], 0) + jnp.where(row >= TH, mask_ref[1], 0)
    times = times + jnp.where(col < EW, mask_ref[2], 0) + jnp.where(col >= TW, mask_ref[3], 0)
    times = jnp.concatenate([times.astype(F32), jnp.ones((1, EARLY - OWN), F32)], axis=1)
    shut = shut_row(EARLY, [(0, OWN, 1)] + spans)
    for p in range(PAIRS):
        scores = scores_of(two_heads(q_ref, p), keys_ref[:, LANES * p : LANES * (p + 1)]) + shut
        top = jnp.max(scores, axis=-1, keepdims=True)
        weights = (jnp.exp(scores - top) * times).astype(BF16)
        state_ref[p] = dot(weights, vals_ref[p])
        top_ref[p] = jnp.broadcast_to(top, (2 * OWN, LANES))


def last_kernel(
    mask_ref, win_ref, q_ref, left_ref, right_ref, state_ref, top_ref,
    scale_ref, shift_ref, gate_ref, fscale_ref, fshift_ref,
    kw_ref, vw_ref, ow_ref, pw_ref, blend_ref,
    kept_ref, spill_e_ref, spill_s_ref, spill_c_ref,
    normed_ref, vals_ref, att_ref,
):
    scale, shift = vec(scale_ref), vec(shift_ref)
    one, two = left_ref.shape[0], left_ref.shape[0] + right_ref.shape[0]
    normed_ref[:one] = layer_norm(left_ref[...].astype(F32), scale, shift)
    normed_ref[one:two] = layer_norm(right_ref[...].astype(F32), scale, shift)
    normed_ref[two:] = jnp.zeros((LATE - two, D), BF16)
    normed = normed_ref[...]
    keys = dot(normed, kw_ref[...]).astype(BF16)
    values = dot(normed, vw_ref[...]).astype(BF16)
    shut = shut_row(LATE, [(0, one, mask_ref[2]), (one, two, mask_ref[3])])
    first = lax.broadcasted_iota(jnp.int32, (OWN, LANES), 1) < HD
    for p in range(PAIRS):
        vals_ref[:, :LANES] = values[:, LANES * p : LANES * (p + 1)]
        vals_ref[:, LANES:] = jnp.ones((LATE, LANES), BF16)
        scores = scores_of(two_heads(q_ref, p), keys[:, LANES * p : LANES * (p + 1)]) + shut
        before = top_ref[p]
        top = jnp.maximum(before, jnp.max(scores, axis=-1, keepdims=True))
        weights = jnp.exp(scores - top).astype(BF16)
        fade = jnp.exp(before - top)
        new = dot(weights, vals_ref[...])
        out = state_ref[p, :, :LANES] * fade + new[:, :LANES]
        out = out / (state_ref[p, :, LANES:] * fade + new[:, LANES:])
        att_ref[:, LANES * p : LANES * (p + 1)] = jnp.where(first, out[:OWN], out[OWN:]).astype(BF16)

    mixed = win_ref[...].astype(F32) + vec(gate_ref) * dot(att_ref[...], ow_ref[...])
    final = layer_norm(mixed, vec(fscale_ref), vec(fshift_ref))
    patch = scores_of(final, pw_ref[...])
    spread = jnp.concatenate(
        [jnp.broadcast_to(blend_ref[r : r + 1], (WW, WW)) for r in range(WH)], axis=0
    )
    own_row = lax.broadcasted_iota(jnp.int32, (OWN, WW), 0) % WW
    own_col = lax.broadcasted_iota(jnp.int32, (OWN, WW), 1)
    b = jnp.sum(jnp.where(own_row == own_col, spread, 0.0), axis=1, keepdims=True)
    both = jnp.concatenate([b * patch, jnp.broadcast_to(b, (OWN, P_SIZE))], axis=1)
    for r in range(WH):
        at = WW * r
        if r < TH:
            kept_ref[TW * r : TW * (r + 1)] = both[at : at + TW]
            spill_e_ref[EW * r : EW * (r + 1)] = both[at + TW : at + WW]
        else:
            k = r - TH
            spill_s_ref[TW * k : TW * (k + 1)] = both[at : at + TW]
            spill_c_ref[EW * k : EW * (k + 1)] = both[at + TW : at + WW]


def blend_kernel(kept_ref, left_ref, upper_ref, corner_ref, out_ref):
    for y in range(TH):
        row = kept_ref[TW * y : TW * (y + 1)]
        head = left_ref[EW * y : EW * (y + 1)]
        if y < EH:
            row = row + upper_ref[TW * y : TW * (y + 1)]
            head = head + corner_ref[EW * y : EW * (y + 1)]
        row = jnp.concatenate([row[:EW] + head, row[EW:]], axis=0)
        ratio = row[:, :P_SIZE] / row[:, P_SIZE:]
        for x in range(TW):
            out_ref[y : y + 1, P_SIZE * x : P_SIZE * (x + 1)] = ratio[x : x + 1]


VM = pl.BlockSpec(memory_space=pltpu.VMEM)
SM = pl.BlockSpec(memory_space=pltpu.SMEM)
HB = pl.BlockSpec(memory_space=pltpu.HBM)
MB = 1 << 20


def call(kernel, outs, scratch=(), smem=0, limit=None, ins=VM):
    def launch(*args):
        return pl.pallas_call(
            kernel,
            out_shape=[jax.ShapeDtypeStruct(s, d) for s, d in outs],
            in_specs=[SM] * smem + [ins] * (len(args) - smem),
            out_specs=[VM] * len(outs),
            scratch_shapes=list(scratch),
            compiler_params=pltpu.CompilerParams(vmem_limit_bytes=limit),
        )(*args)

    return launch


def block(
    latent, attn_shift, attn_scale, attn_gate, final_shift, final_scale,
    q_weight, k_weight, v_weight, o_weight, out_weight, neighbour_mask, blend_weight,
):
    mask = neighbour_mask.reshape(4)
    right, lower, corner, tile, mid = call(
        pack_kernel,
        [(n, BF16) for n in ((TH * EW, D), (EH * TW, D), (EH * EW, D), (TH * TW, D), (TH * MID, D))],
        limit=4 * MB,
    )(latent)
    right = fetch(right, 0, 1)
    corner = fetch(corner, 1, 1)
    lower = fetch(lower, 1, 0)
    left_early, right_early = fetch(tile, 0, -1), fetch(mid, 0, 1)
    weights = (q_weight, k_weight, v_weight, o_weight)
    qw, kw, vw, ow = call(
        load_kernel,
        [(w.shape, BF16) for w in weights],
        scratch=[pltpu.SemaphoreType.DMA((len(weights), PARTS))],
        limit=MB,
        ins=HB,
    )(*(pltpu.with_memory_space_constraint(w, pltpu.HBM) for w in weights))
    win, to_up, to_down, late = call(
        assemble_kernel,
        [(n, BF16) for n in ((OWN, D), (SIDE, D), (SIDE, D), (WH * EW + EH * MID, D))],
        limit=8 * MB,
    )(tile, right, lower, corner)
    left_late, right_late = fetch(lower, 0, -1), fetch(late, 0, 1)
    from_up, from_down = fetch(to_down, -1, 0), fetch(to_up, 1, 0)
    q, k, v = call(own_kernel, [((OWN, AD), BF16)] * 3, limit=12 * MB)(
        win, attn_scale, attn_shift, qw, kw, vw
    )
    state, top = call(
        mid_kernel,
        [((PAIRS, 2 * OWN, 2 * LANES), F32), ((PAIRS, 2 * OWN, LANES), F32)],
        scratch=[
            pltpu.VMEM((EARLY - OWN, D), BF16),
            pltpu.VMEM((EARLY, AD), BF16),
            pltpu.VMEM((PAIRS, EARLY, 2 * LANES), BF16),
        ],
        smem=1,
        limit=20 * MB,
    )(mask, q, k, v, from_up, from_down, left_early, right_early, attn_scale, attn_shift, kw, vw)
    kept, spill_e, spill_s, spill_c = call(
        last_kernel,
        [(n, F32) for n in ((TH * TW, LANES), (TH * EW, LANES), (EH * TW, LANES), (EH * EW, LANES))],
        scratch=[
            pltpu.VMEM((LATE, D), BF16),
            pltpu.VMEM((LATE, 2 * LANES), BF16),
            pltpu.VMEM((OWN, AD), BF16),
        ],
        smem=1,
        limit=16 * MB,
    )(
        mask, win, q, left_late, right_late, state, top,
        attn_scale, attn_shift, attn_gate, final_scale, final_shift,
        kw, vw, ow, out_weight.T, blend_weight,
    )
    left = fetch(spill_e, 0, -1)
    diag = fetch(spill_c, -1, -1)
    upper = fetch(spill_s, -1, 0)
    (out,) = call(blend_kernel, [((TH, TW * P_SIZE), F32)], limit=4 * MB)(kept, left, upper, diag)
    return out


def solution(mesh):
    in_specs = (
        P("row", "col", None),
        P(),
        P(),
        P(),
        P(),
        P(),
        P(),
        P(),
        P(),
        P(),
        P(),
        P("row", "col", None),
        P("row", "col"),
    )
    out_specs = P("row", "col")
    return jax.shard_map(block, mesh=mesh, in_specs=in_specs, out_specs=out_specs, check_vma=False)
```

time: 45.4 us -> 45.8 us (level)
  local copies, waits for them, and re-layouts: 13.3 us -> 1.01 us
  Pallas kernels: 7.54 us -> 13.8 us
  waiting for transfers between devices: 9.43 us -> 14.5 us
  starting transfers between devices: 14.5 us -> 16.1 us
    unnamed x21 -> x18, local copies, waits for them, and re-layouts: 9.76 us -> 1.01 us
    pallas_call x5 -> x7, Pallas kernels: 7.54 us -> 13.8 us  [launch(): pl.pallas_call(kernel, out_shape=[jax.ShapeDtypeStruct(s, d) for s, d in...]
    ppermute x10 -> x12, waiting for transfers between devices: 9.43 us -> 14.5 us  [fetch(): return lax.ppermute(block, ('row', 'col'), route)]
    reshape x5 -> x0, local copies, waits for them, and re-layouts: 3.51 us -> none  [the longest x3 2.1 us: shards(): v.reshape(1, D)]
    ppermute x10 -> x12, starting transfers between devices: 14.5 us -> 16.1 us  [fetch(): return lax.ppermute(block, ('row', 'col'), route)]
  transfers between devices with their start and end apart: 10 -> 12, of which waited for: 2 -> 3; matrix products, arithmetic and copies ran while one was open for 10% -> 0% of each run, Pallas kernels for 3% -> 20%
where the time goes in v2:
time: 45.8 us; the launch traced here: 45.7 us
  starting transfers between devices  16.1 us (35%)
  waiting for transfers between devices  14.5 us (32%)
  Pallas kernels  13.8 us (30%)
  local copies, waits for them, and re-layouts  1.01 us (2%)
    ppermute x12, starting transfers between devices, fetch(): return lax.ppermute(block, ('row', 'col'), route)  16.1 us
    ppermute x12, waiting for transfers between devices, fetch(): return lax.ppermute(block, ('row', 'col'), route)  14.5 us
    pallas_call x7, Pallas kernels, launch(): pl.pallas_call(kernel, out_shape=[jax.ShapeDtypeStruct(s, d) for s, d in...  13.8 us
    unnamed x18, local copies, waits for them, and re-layouts  1.01 us
  transfers between devices with their start and end apart: 12, of which 3 were waited for; matrix products, arithmetic and copies ran while one was open for 0% of the time, Pallas kernels for 20%

profile of v2, /device:TPU:0, one launch (start us, length us, event | category | flops | bytes accessed | tf_op | source)
XLA Modules:
  0.0 45.7 jit_solution(11890450133536206488)
XLA Ops:
  0.0 1.0 %copy-done = bf16[6,12,1536]{2,1,0:T(8,128)(2,1)S(1)} copy-done((bf16[6,12,1536]{2,1,0:T(8,128)(2,1)S(1)}, bf16[6,12,1536]{2,1,0:T(8,128)(2,1)}, u32[]{:S(2)}) %copy-start) | copy-done | bytes 221208
  1.0 6.1 %collective-permute-start = (bf16[24,1536]{1,0:T(8,128)(2,1)S(1)}, bf16[24,1536]{1,0:T(8,128)(2,1)S(1)}, u32[]{:S(2)}, u32[]{:S(2)}) collective-permute-start(bf16[24,1536]{1,0:T(8,128)(2,1)S(1)} %get-tuple-element.28), channel_id=1, source_target_pairs={{1,0},{2,1},{3,2},{4,3},{5,4},{6,5},{7,6},{0,7},{9,8},{10,9},{11,1... | collective-permute-start | bytes 221192 | tf_op jit(solution)/shard_map/ppermute | solution.py:42
  7.1 0.7 %collective-permute-start.1 = (bf16[24,1536]{1,0:T(8,128)(2,1)S(1)}, bf16[24,1536]{1,0:T(8,128)(2,1)S(1)}, u32[]{:S(2)}, u32[]{:S(2)}) collective-permute-start(bf16[24,1536]{1,0:T(8,128)(2,1)S(1)} %get-tuple-element.29), channel_id=1, source_target_pairs={{8,0},{9,1},{10,2},{11,3},{12,4},{13,5},{14,6},{15,7},{16,8},{17,9... | collective-permute-start | bytes 221192 | tf_op jit(solution)/shard_map/ppermute | solution.py:42
  7.8 0.9 %collective-permute-start.2 = (bf16[8,1536]{1,0:T(8,128)(2,1)S(1)}, bf16[8,1536]{1,0:T(8,128)(2,1)S(1)}, u32[]{:S(2)}, u32[]{:S(2)}) collective-permute-start(bf16[8,1536]{1,0:T(8,128)(2,1)S(1)} %get-tuple-element.30), channel_id=1, source_target_pairs={{9,0},{10,1},{11,2},{12,3},{13,4},{14,5},{15,6},{8,7},{17,8},{18,9... | collective-permute-start | bytes 73736 | tf_op jit(solution)/shard_map/ppermute | solution.py:42
  8.7 2.4 %collective-permute-done.2.corner_ref = bf16[8,1536]{1,0:T(8,128)(2,1)S(1)} collective-permute-done((bf16[8,1536]{1,0:T(8,128)(2,1)S(1)}, bf16[8,1536]{1,0:T(8,128)(2,1)S(1)}, u32[]{:S(2)}, u32[]{:S(2)}) %collective-permute-start.2) | collective-permute-done | bytes 24608 | tf_op jit(solution)/shard_map/ppermute | solution.py:42
  11.0 0.1 shard_map.128
  11.1 0.8 %collective-permute-start.5 = (bf16[96,1536]{1,0:T(8,128)(2,1)S(1)}, bf16[96,1536]{1,0:T(8,128)(2,1)S(1)}, u32[]{:S(2)}, u32[]{:S(2)}) collective-permute-start(bf16[96,1536]{1,0:T(8,128)(2,1)S(1)} %get-tuple-element.39), channel_id=1, source_target_pairs={{24,0},{25,1},{26,2},{27,3},{28,4},{29,5},{30,6},{31,7},{0,8},{1,9... | collective-permute-start | bytes 884744 | tf_op jit(solution)/shard_map/ppermute | solution.py:42
  11.9 1.2 %collective-permute-start.6 = (bf16[96,1536]{1,0:T(8,128)(2,1)S(1)}, bf16[96,1536]{1,0:T(8,128)(2,1)S(1)}, u32[]{:S(2)}, u32[]{:S(2)}) collective-permute-start(bf16[96,1536]{1,0:T(8,128)(2,1)S(1)} %get-tuple-element.40), channel_id=1, source_target_pairs={{8,0},{9,1},{10,2},{11,3},{12,4},{13,5},{14,6},{15,7},{16,8},{17,9... | collective-permute-start | bytes 884744 | tf_op jit(solution)/shard_map/ppermute | solution.py:42
  13.1 0.5 %collective-permute-start.7 = (bf16[72,1536]{1,0:T(8,128)(2,1)S(1)}, bf16[72,1536]{1,0:T(8,128)(2,1)S(1)}, u32[]{:S(2)}, u32[]{:S(2)}) collective-permute-start(bf16[72,1536]{1,0:T(8,128)(2,1)S(1)} %get-tuple-element.27.tile_ref), channel_id=1, source_target_pairs={{7,0},{0,1},{1,2},{2,3},{3,4},{4,5},{5,6},{6,7},{15,8},{8,9},{9,10... | collective-permute-start | bytes 663560 | tf_op jit(solution)/shard_map/ppermute | solution.py:42
  13.6 4.2 %collective-permute-start.8 = (bf16[48,1536]{1,0:T(8,128)(2,1)S(1)}, bf16[48,1536]{1,0:T(8,128)(2,1)S(1)}, u32[]{:S(2)}, u32[]{:S(2)}) collective-permute-start(bf16[48,1536]{1,0:T(8,128)(2,1)S(1)} %get-tuple-element.41), channel_id=1, source_target_pairs={{1,0},{2,1},{3,2},{4,3},{5,4},{6,5},{7,6},{0,7},{9,8},{10,9},{11,1... | collective-permute-start | bytes 442376 | tf_op jit(solution)/shard_map/ppermute | solution.py:42
  17.8 0.6 %collective-permute-start.4 = (bf16[48,1536]{1,0:T(8,128)(2,1)S(1)}, bf16[48,1536]{1,0:T(8,128)(2,1)S(1)}, u32[]{:S(2)}, u32[]{:S(2)}) collective-permute-start(bf16[48,1536]{1,0:T(8,128)(2,1)S(1)} %get-tuple-element.36), channel_id=1, source_target_pairs={{1,0},{2,1},{3,2},{4,3},{5,4},{6,5},{7,6},{0,7},{9,8},{10,9},{11,1... | collective-permute-start | bytes 442376 | tf_op jit(solution)/shard_map/ppermute | solution.py:42
  18.4 6.0 %collective-permute-done.8.right_ref = bf16[48,1536]{1,0:T(8,128)(2,1)S(1)} collective-permute-done((bf16[48,1536]{1,0:T(8,128)(2,1)S(1)}, bf16[48,1536]{1,0:T(8,128)(2,1)S(1)}, u32[]{:S(2)}, u32[]{:S(2)}) %collective-permute-start.8) | collective-permute-done | bytes 147488 | tf_op jit(solution)/shard_map/ppermute | solution.py:42
  24.4 3.8 %shard_map.129 = (bf16[1536,768]{1,0:T(8,128)(2,1)S(1)}, bf16[1536,768]{1,0:T(8,128)(2,1)S(1)}, bf16[1536,768]{1,0:T(8,128)(2,1)S(1)}, bf16[768,1536]{1,0:T(8,128)(2,1)S(1)}) custom-call(bf16[1536,768]{1,0:T(8,128)(2,1)} %refs_0_.1, bf16[1536,768]{1,0:T(8,128)(2,1)} %refs_1_.1, bf16[1536,768]{1,0:T(8,128)(2,1)} %refs_2_.1, bf16[768,1536]{1,0:T(8,128)(2,1)} %refs_3_.1), custom_call_target="tpu_custom_call" | custom-call | tf_op jit(solution)/shard_map/pallas_call | solution.py:238
  28.2 0.0 copy-start.8
  28.2 1.3 %shard_map.130 = (bf16[128,768]{1,0:T(8,128)(2,1)S(1)}, bf16[128,768]{1,0:T(8,128)(2,1)S(1)}, bf16[128,768]{1,0:T(8,128)(2,1)S(1)}) custom-call(bf16[128,1536]{1,0:T(8,128)(2,1)S(1)} %get-tuple-element.31.win_ref, f32[1536]{0:T(1024)S(1)} %copy-done.2, f32[1536]{0:T(1024)S(1)} %copy-done.3, bf16[1536,768]{1,0:T(8,128)(2,1)S(1)} %get-tuple-element.32.qw_ref, ...), custom_call_target="tpu_custom_call" | custom-call | tf_op jit(solution)/shard_map/pallas_call | solution.py:238
  29.6 0.0 copy-start.1
  29.7 0.0 copy-start.6
  29.7 4.1 %shard_map.131 = (f32[6,256,256]{2,1,0:T(8,128)S(1)}, f32[6,256,128]{2,1,0:T(8,128)S(1)}) custom-call(s32[4]{0:T(128)S(1)} %bitcast.3, bf16[128,768]{1,0:T(8,128)(2,1)S(1)} %get-tuple-element.35.q_ref, bf16[128,768]{1,0:T(8,128)(2,1)S(1)} %get-tuple-element.37.k_ref, bf16[128,768]{1,0:T(8,128)(2,1)S(1)} %get-tuple-element.38.v_ref, ...), custom_call_target="tpu_custom_call" | custom-call | tf_op jit(solution)/shard_map/pallas_call | solution.py:238
  33.9 3.6 %shard_map.132 = (f32[72,128]{1,0:T(8,128)S(1)}, f32[24,128]{1,0:T(8,128)S(1)}, f32[24,128]{1,0:T(8,128)S(1)}, f32[8,128]{1,0:T(8,128)S(1)}) custom-call(s32[4]{0:T(128)S(1)} %bitcast.4, bf16[128,1536]{1,0:T(8,128)(2,1)S(1)} %get-tuple-element.31.win_ref, bf16[128,768]{1,0:T(8,128)(2,1)S(1)} %get-tuple-element.35.q_ref, ...), custom_call_target="tpu_custom_call" | custom-call | tf_op jit(solution)/shard_map/pallas_call | solution.py:238
  37.5 0.1 collective-permute-start.9
  37.6 0.1 collective-permute-start.10
  37.7 1.1 %collective-permute-start.11 = (f32[8,128]{1,0:T(8,128)S(1)}, f32[8,128]{1,0:T(8,128)S(1)}, u32[]{:S(2)}, u32[]{:S(2)}) collective-permute-start(f32[8,128]{1,0:T(8,128)S(1)} %get-tuple-element.48), channel_id=1, source_target_pairs={{31,0},{24,1},{25,2},{26,3},{27,4},{28,5},{29,6},{30,7},{7,8},{0,9... | collective-permute-start | bytes 12296 | tf_op jit(solution)/shard_map/ppermute | solution.py:42
  38.8 6.1 %collective-permute-done.11.corner_ref = f32[8,128]{1,0:T(8,128)S(1)} collective-permute-done((f32[8,128]{1,0:T(8,128)S(1)}, f32[8,128]{1,0:T(8,128)S(1)}, u32[]{:S(2)}, u32[]{:S(2)}) %collective-permute-start.11) | collective-permute-done | bytes 4128 | tf_op jit(solution)/shard_map/ppermute | solution.py:42
  44.9 0.8 %shard_map.133 = f32[6,768]{1,0:T(8,128)} custom-call(f32[72,128]{1,0:T(8,128)S(1)} %get-tuple-element.45.kept_ref, f32[24,128]{1,0:T(8,128)S(1)} %collective-permute-done.9.left_ref, f32[24,128]{1,0:T(8,128)S(1)} %collective-permute-done.10.upper_ref, f32[8,128]{1,0:T(8,128)S(1)} %collective-permute-done.11.corner_ref), custom_call_target="tpu_custom_call" | custom-call | tf_op jit(solution)/shard_map/pallas_call | solution.py:238
  (25 shorter events, 0.1 us)
Async XLA Ops:
  0.0 1.0 %copy-start = (bf16[6,12,1536]{2,1,0:T(8,128)(2,1)S(1)}, bf16[6,12,1536]{2,1,0:T(8,128)(2,1)}, u32[]{:S(2)}) copy-start(bf16[6,12,1536]{2,1,0:T(8,128)(2,1)} %x_ref.1) | copy-start | bytes 663556
  1.0 10.0 %collective-permute-start = (bf16[24,1536]{1,0:T(8,128)(2,1)S(1)}, bf16[24,1536]{1,0:T(8,128)(2,1)S(1)}, u32[]{:S(2)}, u32[]{:S(2)}) collective-permute-start(bf16[24,1536]{1,0:T(8,128)(2,1)S(1)} %get-tuple-element.28), channel_id=1, source_target_pairs={{1,0},{2,1},{3,2},{4,3},{5,4},{6,5},{7,6},{0,7},{9,8},{10,9},{11,1... | collective-permute-start | bytes 221192 | tf_op jit(solution)/shard_map/ppermute | solution.py:42
  7.1 3.9 %collective-permute-start.1 = (bf16[24,1536]{1,0:T(8,128)(2,1)S(1)}, bf16[24,1536]{1,0:T(8,128)(2,1)S(1)}, u32[]{:S(2)}, u32[]{:S(2)}) collective-permute-start(bf16[24,1536]{1,0:T(8,128)(2,1)S(1)} %get-tuple-element.29), channel_id=1, source_target_pairs={{8,0},{9,1},{10,2},{11,3},{12,4},{13,5},{14,6},{15,7},{16,8},{17,9... | collective-permute-start | bytes 221192 | tf_op jit(solution)/shard_map/ppermute | solution.py:42
  7.8 3.3 %collective-permute-start.2 = (bf16[8,1536]{1,0:T(8,128)(2,1)S(1)}, bf16[8,1536]{1,0:T(8,128)(2,1)S(1)}, u32[]{:S(2)}, u32[]{:S(2)}) collective-permute-start(bf16[8,1536]{1,0:T(8,128)(2,1)S(1)} %get-tuple-element.30), channel_id=1, source_target_pairs={{9,0},{10,1},{11,2},{12,3},{13,4},{14,5},{15,6},{8,7},{17,8},{18,9... | collective-permute-start | bytes 73736 | tf_op jit(solution)/shard_map/ppermute | solution.py:42
  11.1 18.5 %collective-permute-start.5 = (bf16[96,1536]{1,0:T(8,128)(2,1)S(1)}, bf16[96,1536]{1,0:T(8,128)(2,1)S(1)}, u32[]{:S(2)}, u32[]{:S(2)}) collective-permute-start(bf16[96,1536]{1,0:T(8,128)(2,1)S(1)} %get-tuple-element.39), channel_id=1, source_target_pairs={{24,0},{25,1},{26,2},{27,3},{28,4},{29,5},{30,6},{31,7},{0,8},{1,9... | collective-permute-start | bytes 884744 | tf_op jit(solution)/shard_map/ppermute | solution.py:42
  11.9 17.7 %collective-permute-start.6 = (bf16[96,1536]{1,0:T(8,128)(2,1)S(1)}, bf16[96,1536]{1,0:T(8,128)(2,1)S(1)}, u32[]{:S(2)}, u32[]{:S(2)}) collective-permute-start(bf16[96,1536]{1,0:T(8,128)(2,1)S(1)} %get-tuple-element.40), channel_id=1, source_target_pairs={{8,0},{9,1},{10,2},{11,3},{12,4},{13,5},{14,6},{15,7},{16,8},{17,9... | collective-permute-start | bytes 884744 | tf_op jit(solution)/shard_map/ppermute | solution.py:42
  13.1 16.5 %collective-permute-start.7 = (bf16[72,1536]{1,0:T(8,128)(2,1)S(1)}, bf16[72,1536]{1,0:T(8,128)(2,1)S(1)}, u32[]{:S(2)}, u32[]{:S(2)}) collective-permute-start(bf16[72,1536]{1,0:T(8,128)(2,1)S(1)} %get-tuple-element.27.tile_ref), channel_id=1, source_target_pairs={{7,0},{0,1},{1,2},{2,3},{3,4},{4,5},{5,6},{6,7},{15,8},{8,9},{9,10... | collective-permute-start | bytes 663560 | tf_op jit(solution)/shard_map/ppermute | solution.py:42
  13.6 10.8 %collective-permute-start.8 = (bf16[48,1536]{1,0:T(8,128)(2,1)S(1)}, bf16[48,1536]{1,0:T(8,128)(2,1)S(1)}, u32[]{:S(2)}, u32[]{:S(2)}) collective-permute-start(bf16[48,1536]{1,0:T(8,128)(2,1)S(1)} %get-tuple-element.41), channel_id=1, source_target_pairs={{1,0},{2,1},{3,2},{4,3},{5,4},{6,5},{7,6},{0,7},{9,8},{10,9},{11,1... | collective-permute-start | bytes 442376 | tf_op jit(solution)/shard_map/ppermute | solution.py:42
  17.8 10.4 %copy-start.2 = (f32[1536]{0:T(1024)S(1)}, f32[1536]{0:T(1024)}, u32[]{:S(2)}) copy-start(f32[1536]{0:T(1024)} %scale_ref.5) | copy-start | bytes 18436
  17.8 10.4 %copy-start.3 = (f32[1536]{0:T(1024)S(1)}, f32[1536]{0:T(1024)}, u32[]{:S(2)}) copy-start(f32[1536]{0:T(1024)} %shift_ref.5) | copy-start | bytes 18436
  17.8 16.1 %collective-permute-start.4 = (bf16[48,1536]{1,0:T(8,128)(2,1)S(1)}, bf16[48,1536]{1,0:T(8,128)(2,1)S(1)}, u32[]{:S(2)}, u32[]{:S(2)}) collective-permute-start(bf16[48,1536]{1,0:T(8,128)(2,1)S(1)} %get-tuple-element.36), channel_id=1, source_target_pairs={{1,0},{2,1},{3,2},{4,3},{5,4},{6,5},{7,6},{0,7},{9,8},{10,9},{11,1... | collective-permute-start | bytes 442376 | tf_op jit(solution)/shard_map/ppermute | solution.py:42
  24.4 9.5 %collective-permute-start.3 = (bf16[24,1536]{1,0:T(8,128)(2,1)S(1)}, bf16[24,1536]{1,0:T(8,128)(2,1)S(1)}, u32[]{:S(2)}, u32[]{:S(2)}) collective-permute-start(bf16[24,1536]{1,0:T(8,128)(2,1)S(1)} %collective-permute-done.1.lower_ref), channel_id=1, source_target_pairs={{7,0},{0,1},{1,2},{2,3},{3,4},{4,5},{5,6},{6,7},{15,8},{8,9},{9,10... | collective-permute-start | bytes 221192 | tf_op jit(solution)/shard_map/ppermute | solution.py:42
  28.2 1.4 %copy-start.8 = (s32[1,1,4]{2,1,0:T(1,128)S(1)}, s32[1,1,4]{2,1,0:T(1,128)}, u32[]{:S(2)}) copy-start(s32[1,1,4]{2,1,0:T(1,128)} %param.24) | copy-start | bytes 52
  29.6 4.2 %copy-start.1 = (bf16[1536,64]{0,1:T(8,128)(2,1)S(1)}, bf16[1536,64]{0,1:T(8,128)(2,1)}, u32[]{:S(2)}) copy-start(bf16[1536,64]{0,1:T(8,128)(2,1)} %param.23) | copy-start | bytes 589828
  29.6 4.2 %copy-start.4 = (f32[1536]{0:T(1024)S(1)}, f32[1536]{0:T(1024)}, u32[]{:S(2)}) copy-start(f32[1536]{0:T(1024)} %gate_ref.1) | copy-start | bytes 18436
  29.6 4.2 %copy-start.5 = (f32[1536]{0:T(1024)S(1)}, f32[1536]{0:T(1024)}, u32[]{:S(2)}) copy-start(f32[1536]{0:T(1024)} %fscale_ref.1) | copy-start | bytes 18436
  29.7 4.2 %copy-start.6 = (f32[1536]{0:T(1024)S(1)}, f32[1536]{0:T(1024)}, u32[]{:S(2)}) copy-start(f32[1536]{0:T(1024)} %fshift_ref.1) | copy-start | bytes 18436
  29.7 4.2 %copy-start.7 = (f32[8,16]{1,0:T(8,128)S(1)}, f32[8,16]{1,0:T(8,128)}, u32[]{:S(2)}) copy-start(f32[8,16]{1,0:T(8,128)} %blend_ref.1) | copy-start | bytes 1540
  37.5 7.3 %collective-permute-start.9 = (f32[24,128]{1,0:T(8,128)S(1)}, f32[24,128]{1,0:T(8,128)S(1)}, u32[]{:S(2)}, u32[]{:S(2)}) collective-permute-start(f32[24,128]{1,0:T(8,128)S(1)} %get-tuple-element.46), channel_id=1, source_target_pairs={{7,0},{0,1},{1,2},{2,3},{3,4},{4,5},{5,6},{6,7},{15,8},{8,9},{9,10... | collective-permute-start | bytes 36872 | tf_op jit(solution)/shard_map/ppermute | solution.py:42
  37.6 7.3 %collective-permute-start.10 = (f32[24,128]{1,0:T(8,128)S(1)}, f32[24,128]{1,0:T(8,128)S(1)}, u32[]{:S(2)}, u32[]{:S(2)}) collective-permute-start(f32[24,128]{1,0:T(8,128)S(1)} %get-tuple-element.47), channel_id=1, source_target_pairs={{24,0},{25,1},{26,2},{27,3},{28,4},{29,5},{30,6},{31,7},{0,8},{1,9... | collective-permute-start | bytes 36872 | tf_op jit(solution)/shard_map/ppermute | solution.py:42
  37.7 7.2 %collective-permute-start.11 = (f32[8,128]{1,0:T(8,128)S(1)}, f32[8,128]{1,0:T(8,128)S(1)}, u32[]{:S(2)}, u32[]{:S(2)}) collective-permute-start(f32[8,128]{1,0:T(8,128)S(1)} %get-tuple-element.48), channel_id=1, source_target_pairs={{31,0},{24,1},{25,2},{26,3},{27,4},{28,5},{29,6},{30,7},{7,8},{0,9... | collective-permute-start | bytes 12296 | tf_op jit(solution)/shard_map/ppermute | solution.py:42

commit v3 on v0

v3 whole, which is shorter than its diff:
```python
import jax
import jax.numpy as jnp
import numpy as np
from jax import lax
from jax.experimental import pallas as pl
from jax.experimental.pallas import tpu as pltpu
from jax.sharding import PartitionSpec as P


D = 1536
HD = 64
HEADS = 12
P_SIZE = 64
TH = 6
TW = 12
EH = 2
EW = 4
WH = 8
WW = 16
AD = HEADS * HD
PAIRS = HEADS // 2
LANES = 128
OWN = WH * WW
TILE = TH * TW
SIDE = TH * EW
TOP = EH * TW
CORNER = EH * EW
REST = TILE - TOP
RELAY = SIDE + EH * (TW - EW) + CORNER + TOP
EARLY = TILE + 2 * TILE + SIDE + TILE + TOP + TOP
LATE = RELAY + SIDE + REST + CORNER
KEYS = EARLY + LATE

EPSILON = 1e-06
BLOCKED = -1e30
F32 = jnp.float32
BF16 = jnp.bfloat16
MB = 1 << 20


def grid(rows, cols):
    return [(r, c) for r in rows for c in cols]


def places():
    tile_r, top_r, rest_r = range(TH), range(EH), range(EH, TH)
    tile_c, edge_c, body_c = range(TW), range(EW), range(EW, TW)

    def shift(cells, down, right):
        return [(r + down, c + right) for r, c in cells]

    tile, top = grid(tile_r, tile_c), grid(top_r, tile_c)
    packed = grid(tile_r, edge_c) + grid(tile_r, body_c)
    side, corner = grid(tile_r, edge_c), grid(top_r, edge_c)
    relay = shift(packed[: SIDE + EH * (TW - EW)], 0, TW) + shift(corner, 0, 2 * TW) + shift(top, 0, -TW)
    return (
        tile
        + shift(packed, 0, TW)
        + shift(tile, TH, 0)
        + shift(side, 0, 2 * TW)
        + shift(tile, -TH, 0)
        + shift(top, 2 * TH, 0)
        + shift(top, 0, -TW)
        + shift(relay, TH, 0)
        + shift(side, -TH, TW)
        + shift(grid(rest_r, tile_c), 0, -TW)
        + shift(corner, 2 * TH, TW)
    )


def coverage():
    table = np.zeros((8, KEYS), np.float32)
    cells = places()
    assert len(set(cells)) == len(cells) == KEYS
    for j, (down, right) in enumerate(((0, 0), (-TH, 0), (TH, 0), (0, -TW), (0, TW))):
        for k, (r, c) in enumerate(cells):
            table[j, k] = 0 <= r - down < WH and 0 <= c - right < WW
    assert table.sum() == 5 * OWN
    return table


def query_columns():
    cells = grid(range(TH), range(TW)) + grid(range(TH), range(TW, WW))
    cells += grid(range(TH, WH), range(TW)) + grid(range(TH, WH), range(TW, WW))
    return np.eye(WW, dtype=np.float32)[[c for _, c in cells]]


def fetch(block, down, right):
    n_row, n_col = lax.axis_size("row"), lax.axis_size("col")
    route = [
        (((r + down) % n_row) * n_col + (c + right) % n_col, r * n_col + c)
        for r in range(n_row)
        for c in range(n_col)
    ]
    return lax.ppermute(block, ("row", "col"), route)


def vec(ref):
    return ref[...].reshape(1, D)


def layer_norm(features, scale, shift):
    center = features - jnp.mean(features, axis=-1, keepdims=True)
    spread = jnp.mean(center * center, axis=-1, keepdims=True)
    normed = center * lax.rsqrt(spread + EPSILON)
    return (normed * (1.0 + scale) + shift).astype(BF16)


def dot(a, b):
    return jnp.dot(a, b, preferred_element_type=F32)


def dot_t(a, b):
    return lax.dot_general(a, b, (((1,), (1,)), ((), ())), preferred_element_type=F32)


def query(normed, qw_ref):
    return dot(normed, qw_ref[...]).astype(BF16) * BF16(HD**-0.5)


def pack_kernel(x_ref, tile_ref, top_ref, rest_ref, packed_ref, side_ref):
    mid = TW - EW
    for r in range(TH):
        row = x_ref[r]
        tile_ref[TW * r : TW * (r + 1)] = row
        if r < EH:
            top_ref[TW * r : TW * (r + 1)] = row
        else:
            rest_ref[TW * (r - EH) : TW * (r - EH + 1)] = row
        side_ref[EW * r : EW * (r + 1)] = row[:EW]
        packed_ref[EW * r : EW * (r + 1)] = row[:EW]
        packed_ref[SIDE + mid * r : SIDE + mid * (r + 1)] = row[EW:]


def relay_kernel(east_ref, far_ref, top_ref, up_ref, down_ref, twice_ref):
    cut = SIDE + EH * (TW - EW)
    up_ref[:cut] = east_ref[:cut]
    up_ref[cut : cut + CORNER] = far_ref[:CORNER]
    up_ref[cut + CORNER :] = top_ref[...]
    down_ref[...] = east_ref[:SIDE]
    twice_ref[...] = east_ref[:CORNER]


def own_kernel(tile_ref, scale_ref, shift_ref, qw_ref, kw_ref, vw_ref, q_ref, k_ref, v_ref):
    normed = layer_norm(tile_ref[...].astype(F32), vec(scale_ref), vec(shift_ref))
    q_ref[...] = query(normed, qw_ref)
    k_ref[...] = dot(normed, kw_ref[...]).astype(BF16)
    v_ref[...] = dot(normed, vw_ref[...]).astype(BF16)


def norm_blocks(blocks, normed_ref, scale, shift):
    at = 0
    for block in blocks:
        size = block.shape[0]
        normed_ref[at : at + size] = layer_norm(block[...].astype(F32), scale, shift)
        at += size


def mid_kernel(
    east_ref, south_ref, far_ref, north_ref, low_ref, west_ref,
    scale_ref, shift_ref, qw_ref, kw_ref, vw_ref,
    q_ref, k_ref, v_ref,
    normed_ref,
):
    blocks = (east_ref, south_ref, far_ref, north_ref, low_ref, west_ref)
    norm_blocks(blocks, normed_ref, vec(scale_ref), vec(shift_ref))
    normed = normed_ref[...]
    k_ref[...] = dot(normed, kw_ref[...]).astype(BF16)
    v_ref[...] = dot(normed, vw_ref[...]).astype(BF16)
    halo = jnp.concatenate([normed_ref[:SIDE], normed_ref[TILE : TILE + TOP]], axis=0)
    q_ref[...] = query(halo, qw_ref)


def last_kernel(
    mask_ref, cover_ref, pick_ref, tile_ref, east_ref, south_ref,
    relay_ref, side_ref, rest_ref, corner_ref,
    q0_ref, k0_ref, v0_ref, q1_ref, k1_ref, v1_ref,
    scale_ref, shift_ref, gate_ref, fscale_ref, fshift_ref,
    qw_ref, kw_ref, vw_ref, ow_ref, pw_ref, blend_ref,
    kept_ref, spill_e_ref, spill_s_ref, spill_c_ref,
    normed_ref, queries_ref, keys_ref, vals_ref, att_ref,
):
    norm_blocks((relay_ref, side_ref, rest_ref, corner_ref), normed_ref, vec(scale_ref), vec(shift_ref))
    normed = normed_ref[...]
    queries_ref[:TILE] = q0_ref[...]
    queries_ref[TILE : OWN - CORNER] = q1_ref[...]
    queries_ref[OWN - CORNER :] = query(normed_ref[: 2 * CORNER], qw_ref)[:CORNER]
    keys_ref[:TILE] = k0_ref[...]
    keys_ref[TILE:EARLY] = k1_ref[...]
    keys_ref[EARLY:] = dot(normed, kw_ref[...]).astype(BF16)
    values = dot(normed, vw_ref[...]).astype(BF16)

    times = cover_ref[0:1]
    for j in range(4):
        times = times + cover_ref[j + 1 : j + 2] * (mask_ref[j] > 0).astype(F32)
    shut = jnp.where(times > 0, 0.0, BLOCKED)
    lane = lax.broadcasted_iota(jnp.int32, (OWN, LANES), 1)
    for p in range(PAIRS):
        at = slice(LANES * p, LANES * (p + 1))
        vals_ref[:TILE, :LANES] = v0_ref[:, at]
        vals_ref[TILE:EARLY, :LANES] = v1_ref[:, at]
        vals_ref[EARLY:, :LANES] = values[:, at]
        if p == 0:
            vals_ref[:, LANES:] = jnp.ones((KEYS, LANES), BF16)
        q = queries_ref[:, at]
        zero = jnp.zeros_like(q)
        both = jnp.concatenate([jnp.where(lane < HD, q, zero), jnp.where(lane < HD, zero, q)], axis=0)
        scores = dot_t(both, keys_ref[:, at]) + shut
        top = jnp.max(scores, axis=-1, keepdims=True)
        weights = (jnp.exp(scores - top) * times).astype(BF16)
        out = dot(weights, vals_ref[...])
        out = out[:, :LANES] / out[:, LANES:]
        att_ref[:, at] = jnp.where(lane < HD, out[:OWN], out[OWN:]).astype(BF16)

    window = jnp.concatenate(
        [tile_ref[...], east_ref[:SIDE], south_ref[:TOP], relay_ref[:CORNER]], axis=0
    )
    mixed = window.astype(F32) + vec(gate_ref) * dot(att_ref[...], ow_ref[...])
    final = layer_norm(mixed, vec(fscale_ref), vec(fshift_ref))
    patch = dot_t(final, pw_ref[...])
    spans = [(r, TW) for r in range(TH)] + [(r, EW) for r in range(TH)]
    spans += [(r, TW) for r in range(TH, WH)] + [(r, EW) for r in range(TH, WH)]
    spread = jnp.concatenate(
        [jnp.broadcast_to(blend_ref[r : r + 1], (n, WW)) for r, n in spans], axis=0
    )
    b = jnp.sum(spread * pick_ref[...], axis=1, keepdims=True)
    both = jnp.concatenate([b * patch, jnp.broadcast_to(b, (OWN, P_SIZE))], axis=1)
    kept_ref[...] = both[:TILE]
    spill_e_ref[...] = both[TILE : TILE + SIDE]
    spill_s_ref[...] = both[TILE + SIDE : OWN - CORNER]
    spill_c_ref[...] = both[OWN - CORNER :]


def blend_kernel(kept_ref, left_ref, upper_ref, corner_ref, out_ref):
    for y in range(TH):
        row = kept_ref[TW * y : TW * (y + 1)]
        head = left_ref[EW * y : EW * (y + 1)]
        if y < EH:
            row = row + upper_ref[TW * y : TW * (y + 1)]
            head = head + corner_ref[EW * y : EW * (y + 1)]
        row = jnp.concatenate([row[:EW] + head, row[EW:]], axis=0)
        ratio = row[:, :P_SIZE] / row[:, P_SIZE:]
        for x in range(TW):
            out_ref[y : y + 1, P_SIZE * x : P_SIZE * (x + 1)] = ratio[x : x + 1]


VM = pl.BlockSpec(memory_space=pltpu.VMEM)
SM = pl.BlockSpec(memory_space=pltpu.SMEM)


def call(kernel, outs, *args, scratch=(), smem=0, limit=None, flops=0):
    cost = pl.CostEstimate(flops=flops, bytes_accessed=0, transcendentals=0) if flops else None
    return pl.pallas_call(
        kernel,
        out_shape=[jax.ShapeDtypeStruct(s, d) for s, d in outs],
        in_specs=[SM] * smem + [VM] * (len(args) - smem),
        out_specs=[VM] * len(outs),
        scratch_shapes=[pltpu.VMEM(s, d) for s, d in scratch],
        compiler_params=pltpu.CompilerParams(vmem_limit_bytes=limit),
        cost_estimate=cost,
    )(*args)


def block(
    latent,
    attn_shift,
    attn_scale,
    attn_gate,
    final_shift,
    final_scale,
    q_weight,
    k_weight,
    v_weight,
    o_weight,
    out_weight,
    neighbour_mask,
    blend_weight,
):
    mask = neighbour_mask.reshape(4)
    tile, top, rest, packed, side = call(
        pack_kernel,
        [((n, D), BF16) for n in (TILE, TOP, REST, TILE, SIDE)],
        latent,
        limit=4 * MB,
        flops=1 << 33,
    )
    east, far = fetch(packed, 0, 1), fetch(side, 0, 2)
    west_top, west_rest = fetch(top, 0, -1), fetch(rest, 0, -1)
    north, south = fetch(tile, -1, 0), fetch(tile, 1, 0)
    low = fetch(top, 2, 0)
    q0, k0, v0 = call(
        own_kernel,
        [((TILE, AD), BF16)] * 3,
        tile, attn_scale, attn_shift, q_weight, k_weight, v_weight,
        limit=8 * MB,
    )
    to_up, to_down, to_twice = call(
        relay_kernel,
        [((n, D), BF16) for n in (RELAY, SIDE, CORNER)],
        east, far, west_top,
        limit=4 * MB,
    )
    relayed = fetch(to_up, 1, 0)
    north_side = fetch(to_down, -1, 0)
    low_corner = fetch(to_twice, 2, 0)
    q1, k1, v1 = call(
        mid_kernel,
        [((n, AD), BF16) for n in (SIDE + TOP, EARLY - TILE, EARLY - TILE)],
        east, south, far, north, low, west_top,
        attn_scale, attn_shift, q_weight, k_weight, v_weight,
        scratch=[((EARLY - TILE, D), BF16)],
        limit=12 * MB,
    )
    kept, spill_e, spill_s, spill_c = call(
        last_kernel,
        [((n, LANES), F32) for n in (TILE, SIDE, TOP, CORNER)],
        mask, jnp.asarray(coverage()), jnp.asarray(query_columns()), tile, east, south,
        relayed, north_side, west_rest, low_corner,
        q0, k0, v0, q1, k1, v1,
        attn_scale, attn_shift, attn_gate, final_scale, final_shift,
        q_weight, k_weight, v_weight, o_weight, out_weight.T, blend_weight,
        scratch=[
            ((LATE, D), BF16),
            ((OWN, AD), BF16),
            ((KEYS, AD), BF16),
            ((KEYS, 2 * LANES), BF16),
            ((OWN, AD), BF16),
        ],
        smem=1,
        limit=20 * MB,
    )
    left = fetch(spill_e, 0, -1)
    diag = fetch(spill_c, -1, -1)
    upper = fetch(spill_s, -1, 0)
    (out,) = call(blend_kernel, [((TH, TW * P_SIZE), F32)], kept, left, upper, diag, limit=4 * MB)
    return out


def solution(mesh):
    in_specs = (
        P("row", "col", None),
        P(),
        P(),
        P(),
        P(),
        P(),
        P(),
        P(),
        P(),
        P(),
        P(),
        P("row", "col", None),
        P("row", "col"),
    )
    out_specs = P("row", "col")
    return jax.shard_map(block, mesh=mesh, in_specs=in_specs, out_specs=out_specs, check_vma=False)
```

time: 93.4 us -> 42.1 us (0.45); the launches traced: 92.3 us -> 42 us
  matrix products: 26.2 us -> 0 us
  local copies, waits for them, and re-layouts: 19.6 us -> 1.18 us
  other arithmetic: 16.7 us -> 0 us
  waiting for transfers between devices: 7.14 us -> 17.4 us
  Pallas kernels: 0 us -> 9.2 us
  starting transfers between devices: 19.7 us -> 13.9 us
  between operations: 3.01 us -> 0.25 us
    dot_general x15 -> x0, matrix products: 26.2 us -> none  [the longest x5 11 us: partial_state(): jnp.einsum('hqk,khd->qhd', exp_scores.astype(jnp.bfloat16), value_h, pref...]
    ppermute x8 -> x0, local copies, waits for them, and re-layouts: 11.3 us -> none  [from_behind(): return lax.ppermute(block, axis, route)]
    ppermute x14 -> x13, waiting for transfers between devices: 7.14 us -> 17.4 us  [fetch(): return lax.ppermute(block, ('row', 'col'), route)]
    pallas_call x0 -> x6, Pallas kernels: none -> 9.2 us  [call(): pl.pallas_call(kernel, out_shape=[jax.ShapeDtypeStruct(s, d) for s, d in...]
    ppermute x14 -> x13, starting transfers between devices: 19.7 us -> 13.9 us  [fetch(): return lax.ppermute(block, ('row', 'col'), route)]
    reduce_sum x6 -> x0, other arithmetic: 5.47 us -> none  [the longest x3 2.88 us: partial_state(): row_mass = jnp.sum(exp_scores, axis=-1)]
    add x3 -> x0, other arithmetic: 5.25 us -> none  [the longest x1 3.25 us: merge_state(): row_mass = earlier[1] * scale_a + second[1] * scale_b]
    convert_element_type x3 -> x0, local copies, waits for them, and re-layouts: 3.66 us -> none  [the longest x1 1.76 us: shards(): jnp.dot(normed, k_weight, preferred_element_type=jnp.float32)]
  transfers between devices with their start and end apart: 14 -> 13, of which waited for: 2 -> 3; matrix products, arithmetic and copies ran while one was open for 65% -> 0% of each run, Pallas kernels for 0% -> 9%
where the time goes in v3:
time: 42.1 us; the launch traced here: 42 us
  waiting for transfers between devices  17.4 us (41%)
  starting transfers between devices  13.9 us (33%)
  Pallas kernels  9.2 us (22%)
  local copies, waits for them, and re-layouts  1.18 us (3%)
    ppermute x13, waiting for transfers between devices, fetch(): return lax.ppermute(block, ('row', 'col'), route)  17.4 us
    ppermute x13, starting transfers between devices, fetch(): return lax.ppermute(block, ('row', 'col'), route)  13.9 us
    pallas_call x6, Pallas kernels, call(): pl.pallas_call(kernel, out_shape=[jax.ShapeDtypeStruct(s, d) for s, d in...  9.2 us
    unnamed x30, local copies, waits for them, and re-layouts  1.18 us
  transfers between devices with their start and end apart: 13, of which 3 were waited for; matrix products, arithmetic and copies ran while one was open for 0% of the time, Pallas kernels for 9%

profile of v3, /device:TPU:0, one launch (start us, length us, event | category | flops | bytes accessed | tf_op | source)
XLA Modules:
  0.0 42.0 jit_solution(5093735816769266482)
XLA Ops:
  0.0 1.1 %copy-done.14 = bf16[6,12,1536]{2,1,0:T(8,128)(2,1)S(1)} copy-done((bf16[6,12,1536]{2,1,0:T(8,128)(2,1)S(1)}, bf16[6,12,1536]{2,1,0:T(8,128)(2,1)}, u32[]{:S(2)}) %copy-start.14) | copy-done | bytes 221208
  1.1 0.1 shard_map.145
  1.2 6.1 %collective-permute-start = (bf16[72,1536]{1,0:T(8,128)(2,1)S(1)}, bf16[72,1536]{1,0:T(8,128)(2,1)S(1)}, u32[]{:S(2)}, u32[]{:S(2)}) collective-permute-start(bf16[72,1536]{1,0:T(8,128)(2,1)S(1)} %get-tuple-element.24), channel_id=1, source_target_pairs={{1,0},{2,1},{3,2},{4,3},{5,4},{6,5},{7,6},{0,7},{9,8},{10,9},{11,1... | collective-permute-start | bytes 663560 | tf_op jit(solution)/shard_map/ppermute | solution.py:95
  7.3 1.1 %collective-permute-start.2 = (bf16[24,1536]{1,0:T(8,128)(2,1)S(1)}, bf16[24,1536]{1,0:T(8,128)(2,1)S(1)}, u32[]{:S(2)}, u32[]{:S(2)}) collective-permute-start(bf16[24,1536]{1,0:T(8,128)(2,1)S(1)} %get-tuple-element.25), channel_id=1, source_target_pairs={{2,0},{3,1},{4,2},{5,3},{6,4},{7,5},{0,6},{1,7},{10,8},{11,9},{12,... | collective-permute-start | bytes 221192 | tf_op jit(solution)/shard_map/ppermute | solution.py:95
  8.4 0.1 collective-permute-start.1
  8.5 0.4 collective-permute-start.8
  8.9 5.6 %collective-permute-done.3.top_ref.west_ref = bf16[24,1536]{1,0:T(8,128)(2,1)S(1)} collective-permute-done((bf16[24,1536]{1,0:T(8,128)(2,1)S(1)}, bf16[24,1536]{1,0:T(8,128)(2,1)S(1)}, u32[]{:S(2)}, u32[]{:S(2)}) %collective-permute-start.3) | collective-permute-done | bytes 73760 | tf_op jit(solution)/shard_map/ppermute | solution.py:95
  14.5 0.1 collective-permute-start.4
  14.6 1.6 %collective-permute-start.9 = (bf16[24,1536]{1,0:T(8,128)(2,1)S(1)}, bf16[24,1536]{1,0:T(8,128)(2,1)S(1)}, u32[]{:S(2)}, u32[]{:S(2)}) collective-permute-start(bf16[24,1536]{1,0:T(8,128)(2,1)S(1)} %get-tuple-element.26), channel_id=1, source_target_pairs={{16,0},{17,1},{18,2},{19,3},{20,4},{21,5},{22,6},{23,7},{24,8},{25... | collective-permute-start | bytes 221192 | tf_op jit(solution)/shard_map/ppermute | solution.py:95
  16.2 0.1 collective-permute-start.6
  16.2 5.4 %collective-permute-done.9.low_ref = bf16[24,1536]{1,0:T(8,128)(2,1)S(1)} collective-permute-done((bf16[24,1536]{1,0:T(8,128)(2,1)S(1)}, bf16[24,1536]{1,0:T(8,128)(2,1)S(1)}, u32[]{:S(2)}, u32[]{:S(2)}) %collective-permute-start.9) | collective-permute-done | bytes 73760 | tf_op jit(solution)/shard_map/ppermute | solution.py:95
  21.6 0.5 %collective-permute-start.7 = (bf16[8,1536]{1,0:T(8,128)(2,1)S(1)}, bf16[8,1536]{1,0:T(8,128)(2,1)S(1)}, u32[]{:S(2)}, u32[]{:S(2)}) collective-permute-start(bf16[8,1536]{1,0:T(8,128)(2,1)S(1)} %get-tuple-element.30), channel_id=1, source_target_pairs={{16,0},{17,1},{18,2},{19,3},{20,4},{21,5},{22,6},{23,7},{24,8},{25... | collective-permute-start | bytes 73736 | tf_op jit(solution)/shard_map/ppermute | solution.py:95
  22.2 1.5 %shard_map.147 = (bf16[72,768]{1,0:T(8,128)(2,1)S(1)}, bf16[72,768]{1,0:T(8,128)(2,1)S(1)}, bf16[72,768]{1,0:T(8,128)(2,1)S(1)}) custom-call(bf16[72,1536]{1,0:T(8,128)(2,1)S(1)} %get-tuple-element.23.tile_ref, f32[1536]{0:T(1024)S(1)} %copy-done.5, f32[1536]{0:T(1024)S(1)} %copy-done.6, bf16[1536,768]{1,0:T(8,128)(2,1)S(1)} %copy-done, ...), custom_call_target="tpu_custom_call" | custom-call | tf_op jit(solution)/shard_map/pallas_call | solution.py:253
  23.7 0.0 copy-start.3
  23.7 0.0 copy-start.7
  23.7 0.0 copy-start.8
  23.8 0.0 copy-start.9
  23.8 2.4 %shard_map.148 = (bf16[48,768]{1,0:T(8,128)(2,1)S(1)}, bf16[288,768]{1,0:T(8,128)(2,1)S(1)}, bf16[288,768]{1,0:T(8,128)(2,1)S(1)}) custom-call(bf16[72,1536]{1,0:T(8,128)(2,1)S(1)} %collective-permute-done.east_ref, bf16[72,1536]{1,0:T(8,128)(2,1)S(1)} %collective-permute-done.1.south_ref, bf16[24,1536]{1,0:T(8,128)(2,1)S(1)} %collective-permute-done.2.far_ref, ...), custom_call_target="tpu_custom_call" | custom-call | tf_op jit(solution)/shard_map/pallas_call | solution.py:253
  26.3 4.4 %shard_map.149 = (f32[72,128]{1,0:T(8,128)S(1)}, f32[24,128]{1,0:T(8,128)S(1)}, f32[24,128]{1,0:T(8,128)S(1)}, f32[8,128]{1,0:T(8,128)S(1)}) custom-call(s32[4]{0:T(128)S(1)} %bitcast.3, f32[8,512]{1,0:T(8,128)S(1)} %copy-done.8, f32[128,16]{1,0:T(8,128)S(1)} %copy-done.7, bf16[72,1536]{1,0:T(8,128)(2,1)S(1)} %get-tuple-element.23.tile_ref, ...), custom_call_target="tpu_custom_call" | custom-call | tf_op jit(solution)/shard_map/pallas_call | solution.py:253
  30.7 2.9 %collective-permute-start.10 = (f32[24,128]{1,0:T(8,128)S(1)}, f32[24,128]{1,0:T(8,128)S(1)}, u32[]{:S(2)}, u32[]{:S(2)}) collective-permute-start(f32[24,128]{1,0:T(8,128)S(1)} %get-tuple-element.38), channel_id=1, source_target_pairs={{7,0},{0,1},{1,2},{2,3},{3,4},{4,5},{5,6},{6,7},{15,8},{8,9},{9,10... | collective-permute-start | bytes 36872 | tf_op jit(solution)/shard_map/ppermute | solution.py:95
  33.6 1.0 %collective-permute-start.11 = (f32[24,128]{1,0:T(8,128)S(1)}, f32[24,128]{1,0:T(8,128)S(1)}, u32[]{:S(2)}, u32[]{:S(2)}) collective-permute-start(f32[24,128]{1,0:T(8,128)S(1)} %get-tuple-element.39), channel_id=1, source_target_pairs={{24,0},{25,1},{26,2},{27,3},{28,4},{29,5},{30,6},{31,7},{0,8},{1,9... | collective-permute-start | bytes 36872 | tf_op jit(solution)/shard_map/ppermute | solution.py:95
  34.6 0.2 collective-permute-start.12
  34.8 6.4 %collective-permute-done.12.corner_ref = f32[8,128]{1,0:T(8,128)S(1)} collective-permute-done((f32[8,128]{1,0:T(8,128)S(1)}, f32[8,128]{1,0:T(8,128)S(1)}, u32[]{:S(2)}, u32[]{:S(2)}) %collective-permute-start.12) | collective-permute-done | bytes 4128 | tf_op jit(solution)/shard_map/ppermute | solution.py:95
  41.2 0.8 %shard_map.150 = f32[6,768]{1,0:T(8,128)} custom-call(f32[72,128]{1,0:T(8,128)S(1)} %get-tuple-element.37.kept_ref, f32[24,128]{1,0:T(8,128)S(1)} %collective-permute-done.10.left_ref, f32[24,128]{1,0:T(8,128)S(1)} %collective-permute-done.11.upper_ref, f32[8,128]{1,0:T(8,128)S(1)} %collective-permute-done.12.corner_ref), custom_call_target="tpu_custom_call" | custom-call | tf_op jit(solution)/shard_map/pallas_call | solution.py:253
  (38 shorter events, 0.1 us)
Async XLA Ops:
  0.0 22.1 %copy-start.6 = (f32[1536]{0:T(1024)S(1)}, f32[1536]{0:T(1024)}, u32[]{:S(2)}) copy-start(f32[1536]{0:T(1024)} %shift_ref.5) | copy-start | bytes 18436
  0.0 22.1 %copy-start.5 = (f32[1536]{0:T(1024)S(1)}, f32[1536]{0:T(1024)}, u32[]{:S(2)}) copy-start(f32[1536]{0:T(1024)} %scale_ref.5) | copy-start | bytes 18436
  0.0 22.1 %copy-start = (bf16[1536,768]{1,0:T(8,128)(2,1)S(1)}, bf16[1536,768]{1,0:T(8,128)(2,1)}, u32[]{:S(2)}) copy-start(bf16[1536,768]{1,0:T(8,128)(2,1)} %qw_ref.5) | copy-start | bytes 7077892
  0.0 22.1 %copy-start.1 = (bf16[1536,768]{1,0:T(8,128)(2,1)S(1)}, bf16[1536,768]{1,0:T(8,128)(2,1)}, u32[]{:S(2)}) copy-start(bf16[1536,768]{1,0:T(8,128)(2,1)} %kw_ref.5) | copy-start | bytes 7077892
  0.0 22.1 %copy-start.2 = (bf16[1536,768]{1,0:T(8,128)(2,1)S(1)}, bf16[1536,768]{1,0:T(8,128)(2,1)}, u32[]{:S(2)}) copy-start(bf16[1536,768]{1,0:T(8,128)(2,1)} %vw_ref.5) | copy-start | bytes 7077892
  1.2 13.3 %collective-permute-start = (bf16[72,1536]{1,0:T(8,128)(2,1)S(1)}, bf16[72,1536]{1,0:T(8,128)(2,1)S(1)}, u32[]{:S(2)}, u32[]{:S(2)}) collective-permute-start(bf16[72,1536]{1,0:T(8,128)(2,1)S(1)} %get-tuple-element.24), channel_id=1, source_target_pairs={{1,0},{2,1},{3,2},{4,3},{5,4},{6,5},{7,6},{0,7},{9,8},{10,9},{11,1... | collective-permute-start | bytes 663560 | tf_op jit(solution)/shard_map/ppermute | solution.py:95
  7.3 7.2 %collective-permute-start.3 = (bf16[24,1536]{1,0:T(8,128)(2,1)S(1)}, bf16[24,1536]{1,0:T(8,128)(2,1)S(1)}, u32[]{:S(2)}, u32[]{:S(2)}) collective-permute-start(bf16[24,1536]{1,0:T(8,128)(2,1)S(1)} %get-tuple-element.26), channel_id=1, source_target_pairs={{7,0},{0,1},{1,2},{2,3},{3,4},{4,5},{5,6},{6,7},{15,8},{8,9},{9,10... | collective-permute-start | bytes 221192 | tf_op jit(solution)/shard_map/ppermute | solution.py:95
  7.3 7.2 %collective-permute-start.2 = (bf16[24,1536]{1,0:T(8,128)(2,1)S(1)}, bf16[24,1536]{1,0:T(8,128)(2,1)S(1)}, u32[]{:S(2)}, u32[]{:S(2)}) collective-permute-start(bf16[24,1536]{1,0:T(8,128)(2,1)S(1)} %get-tuple-element.25), channel_id=1, source_target_pairs={{2,0},{3,1},{4,2},{5,3},{6,4},{7,5},{0,6},{1,7},{10,8},{11,9},{12,... | collective-permute-start | bytes 221192 | tf_op jit(solution)/shard_map/ppermute | solution.py:95
  8.4 13.2 %collective-permute-start.1 = (bf16[72,1536]{1,0:T(8,128)(2,1)S(1)}, bf16[72,1536]{1,0:T(8,128)(2,1)S(1)}, u32[]{:S(2)}, u32[]{:S(2)}) collective-permute-start(bf16[72,1536]{1,0:T(8,128)(2,1)S(1)} %get-tuple-element.23.tile_ref), channel_id=1, source_target_pairs={{8,0},{9,1},{10,2},{11,3},{12,4},{13,5},{14,6},{15,7},{16,8},{17,9... | collective-permute-start | bytes 663560 | tf_op jit(solution)/shard_map/ppermute | solution.py:95
  8.5 15.4 %collective-permute-start.8 = (bf16[72,1536]{1,0:T(8,128)(2,1)S(1)}, bf16[72,1536]{1,0:T(8,128)(2,1)S(1)}, u32[]{:S(2)}, u32[]{:S(2)}) collective-permute-start(bf16[72,1536]{1,0:T(8,128)(2,1)S(1)} %get-tuple-element.23.tile_ref), channel_id=1, source_target_pairs={{24,0},{25,1},{26,2},{27,3},{28,4},{29,5},{30,6},{31,7},{0,8},{1,9... | collective-permute-start | bytes 663560 | tf_op jit(solution)/shard_map/ppermute | solution.py:95
  14.5 11.7 %collective-permute-start.4 = (bf16[72,1536]{1,0:T(8,128)(2,1)S(1)}, bf16[72,1536]{1,0:T(8,128)(2,1)S(1)}, u32[]{:S(2)}, u32[]{:S(2)}) collective-permute-start(bf16[72,1536]{1,0:T(8,128)(2,1)S(1)} %get-tuple-element.27), channel_id=1, source_target_pairs={{8,0},{9,1},{10,2},{11,3},{12,4},{13,5},{14,6},{15,7},{16,8},{17,9... | collective-permute-start | bytes 663560 | tf_op jit(solution)/shard_map/ppermute | solution.py:95
  14.6 7.0 %collective-permute-start.9 = (bf16[24,1536]{1,0:T(8,128)(2,1)S(1)}, bf16[24,1536]{1,0:T(8,128)(2,1)S(1)}, u32[]{:S(2)}, u32[]{:S(2)}) collective-permute-start(bf16[24,1536]{1,0:T(8,128)(2,1)S(1)} %get-tuple-element.26), channel_id=1, source_target_pairs={{16,0},{17,1},{18,2},{19,3},{20,4},{21,5},{22,6},{23,7},{24,8},{25... | collective-permute-start | bytes 221192 | tf_op jit(solution)/shard_map/ppermute | solution.py:95
  16.2 10.0 %collective-permute-start.6 = (bf16[48,1536]{1,0:T(8,128)(2,1)S(1)}, bf16[48,1536]{1,0:T(8,128)(2,1)S(1)}, u32[]{:S(2)}, u32[]{:S(2)}) collective-permute-start(bf16[48,1536]{1,0:T(8,128)(2,1)S(1)} %get-tuple-element.29), channel_id=1, source_target_pairs={{7,0},{0,1},{1,2},{2,3},{3,4},{4,5},{5,6},{6,7},{15,8},{8,9},{9,10... | collective-permute-start | bytes 442376 | tf_op jit(solution)/shard_map/ppermute | solution.py:95
  21.6 4.6 %collective-permute-start.5 = (bf16[24,1536]{1,0:T(8,128)(2,1)S(1)}, bf16[24,1536]{1,0:T(8,128)(2,1)S(1)}, u32[]{:S(2)}, u32[]{:S(2)}) collective-permute-start(bf16[24,1536]{1,0:T(8,128)(2,1)S(1)} %get-tuple-element.28), channel_id=1, source_target_pairs={{24,0},{25,1},{26,2},{27,3},{28,4},{29,5},{30,6},{31,7},{0,8},{1,9... | collective-permute-start | bytes 221192 | tf_op jit(solution)/shard_map/ppermute | solution.py:95
  21.6 4.6 %collective-permute-start.7 = (bf16[8,1536]{1,0:T(8,128)(2,1)S(1)}, bf16[8,1536]{1,0:T(8,128)(2,1)S(1)}, u32[]{:S(2)}, u32[]{:S(2)}) collective-permute-start(bf16[8,1536]{1,0:T(8,128)(2,1)S(1)} %get-tuple-element.30), channel_id=1, source_target_pairs={{16,0},{17,1},{18,2},{19,3},{20,4},{21,5},{22,6},{23,7},{24,8},{25... | collective-permute-start | bytes 73736 | tf_op jit(solution)/shard_map/ppermute | solution.py:95
  23.7 2.5 %copy-start.3 = (bf16[768,1536]{1,0:T(8,128)(2,1)S(1)}, bf16[768,1536]{1,0:T(8,128)(2,1)}, u32[]{:S(2)}) copy-start(bf16[768,1536]{1,0:T(8,128)(2,1)} %ow_ref.1) | copy-start | bytes 7077892
  23.7 2.5 %copy-start.4 = (bf16[1536,64]{0,1:T(8,128)(2,1)S(1)}, bf16[1536,64]{0,1:T(8,128)(2,1)}, u32[]{:S(2)}) copy-start(bf16[1536,64]{0,1:T(8,128)(2,1)} %param.25) | copy-start | bytes 589828
  23.7 2.5 %copy-start.7 = (f32[128,16]{1,0:T(8,128)S(1)}, f32[128,16]{1,0:T(8,128)}, u32[]{:S(2)}) copy-start(f32[128,16]{1,0:T(8,128)} %constant.5.clone.pick_ref) | copy-start | bytes 24580
  23.7 2.5 %copy-start.8 = (f32[8,512]{1,0:T(8,128)S(1)}, f32[8,512]{1,0:T(8,128)}, u32[]{:S(2)}) copy-start(f32[8,512]{1,0:T(8,128)} %constant.4.clone.cover_ref) | copy-start | bytes 49156
  23.8 2.5 %copy-start.9 = (f32[1536]{0:T(1024)S(1)}, f32[1536]{0:T(1024)}, u32[]{:S(2)}) copy-start(f32[1536]{0:T(1024)} %gate_ref.1) | copy-start | bytes 18436
  23.8 2.5 %copy-start.10 = (f32[1536]{0:T(1024)S(1)}, f32[1536]{0:T(1024)}, u32[]{:S(2)}) copy-start(f32[1536]{0:T(1024)} %fscale_ref.1) | copy-start | bytes 18436
  30.7 10.5 %collective-permute-start.10 = (f32[24,128]{1,0:T(8,128)S(1)}, f32[24,128]{1,0:T(8,128)S(1)}, u32[]{:S(2)}, u32[]{:S(2)}) collective-permute-start(f32[24,128]{1,0:T(8,128)S(1)} %get-tuple-element.38), channel_id=1, source_target_pairs={{7,0},{0,1},{1,2},{2,3},{3,4},{4,5},{5,6},{6,7},{15,8},{8,9},{9,10... | collective-permute-start | bytes 36872 | tf_op jit(solution)/shard_map/ppermute | solution.py:95
  33.6 7.6 %collective-permute-start.11 = (f32[24,128]{1,0:T(8,128)S(1)}, f32[24,128]{1,0:T(8,128)S(1)}, u32[]{:S(2)}, u32[]{:S(2)}) collective-permute-start(f32[24,128]{1,0:T(8,128)S(1)} %get-tuple-element.39), channel_id=1, source_target_pairs={{24,0},{25,1},{26,2},{27,3},{28,4},{29,5},{30,6},{31,7},{0,8},{1,9... | collective-permute-start | bytes 36872 | tf_op jit(solution)/shard_map/ppermute | solution.py:95
  34.6 6.6 %collective-permute-start.12 = (f32[8,128]{1,0:T(8,128)S(1)}, f32[8,128]{1,0:T(8,128)S(1)}, u32[]{:S(2)}, u32[]{:S(2)}) collective-permute-start(f32[8,128]{1,0:T(8,128)S(1)} %get-tuple-element.40), channel_id=1, source_target_pairs={{31,0},{24,1},{25,2},{26,3},{27,4},{28,5},{29,6},{30,7},{7,8},{0,9... | collective-permute-start | bytes 12296 | tf_op jit(solution)/shard_map/ppermute | solution.py:95
  (4 other events, 8.6 us)

commit v4 on v3

--- a/solution.py
+++ b/solution.py
@@ -27,6 +27,7 @@
 CORNER = EH * EW
 REST = TILE - TOP
 RELAY = SIDE + EH * (TW - EW) + CORNER + TOP
+CUT = SIDE + EH * (TW - EW)
 EARLY = TILE + 2 * TILE + SIDE + TILE + TOP + TOP
 LATE = RELAY + SIDE + REST + CORNER
 KEYS = EARLY + LATE
@@ -52,15 +53,16 @@
     tile, top = grid(tile_r, tile_c), grid(top_r, tile_c)
     packed = grid(tile_r, edge_c) + grid(tile_r, body_c)
     side, corner = grid(tile_r, edge_c), grid(top_r, edge_c)
-    relay = shift(packed[: SIDE + EH * (TW - EW)], 0, TW) + shift(corner, 0, 2 * TW) + shift(top, 0, -TW)
+    relay = shift(packed[:CUT], 0, TW) + shift(corner, 0, 2 * TW) + shift(top, 0, -TW)
     return (
         tile
-        + shift(packed, 0, TW)
+        + shift(packed[:CUT], 0, TW)
         + shift(tile, TH, 0)
         + shift(side, 0, 2 * TW)
         + shift(tile, -TH, 0)
         + shift(top, 2 * TH, 0)
         + shift(top, 0, -TW)
+        + shift(packed[CUT:], 0, TW)
         + shift(relay, TH, 0)
         + shift(side, -TH, TW)
         + shift(grid(rest_r, tile_c), 0, -TW)
@@ -118,7 +120,7 @@
     return dot(normed, qw_ref[...]).astype(BF16) * BF16(HD**-0.5)
 
 
-def pack_kernel(x_ref, tile_ref, top_ref, rest_ref, packed_ref, side_ref):
+def pack_kernel(x_ref, tile_ref, top_ref, rest_ref, near_ref, body_ref, side_ref):
     mid = TW - EW
     for r in range(TH):
         row = x_ref[r]
@@ -128,15 +130,17 @@
         else:
             rest_ref[TW * (r - EH) : TW * (r - EH + 1)] = row
         side_ref[EW * r : EW * (r + 1)] = row[:EW]
-        packed_ref[EW * r : EW * (r + 1)] = row[:EW]
-        packed_ref[SIDE + mid * r : SIDE + mid * (r + 1)] = row[EW:]
+        near_ref[EW * r : EW * (r + 1)] = row[:EW]
+        if r < EH:
+            near_ref[SIDE + mid * r : SIDE + mid * (r + 1)] = row[EW:]
+        else:
+            body_ref[mid * (r - EH) : mid * (r - EH + 1)] = row[EW:]
 
 
 def relay_kernel(east_ref, far_ref, top_ref, up_ref, down_ref, twice_ref):
-    cut = SIDE + EH * (TW - EW)
-    up_ref[:cut] = east_ref[:cut]
-    up_ref[cut : cut + CORNER] = far_ref[:CORNER]
-    up_ref[cut + CORNER :] = top_ref[...]
+    up_ref[:CUT] = east_ref[...]
+    up_ref[CUT : CUT + CORNER] = far_ref[:CORNER]
+    up_ref[CUT + CORNER :] = top_ref[...]
     down_ref[...] = east_ref[:SIDE]
     twice_ref[...] = east_ref[:CORNER]
 
@@ -157,78 +161,101 @@
 
 
 def mid_kernel(
-    east_ref, south_ref, far_ref, north_ref, low_ref, west_ref,
+    east_ref, south_ref, far_ref, north_ref, low_ref, west_ref, body_ref,
     scale_ref, shift_ref, qw_ref, kw_ref, vw_ref,
     q_ref, k_ref, v_ref,
     normed_ref,
 ):
-    blocks = (east_ref, south_ref, far_ref, north_ref, low_ref, west_ref)
+    blocks = (east_ref, south_ref, far_ref, north_ref, low_ref, west_ref, body_ref)
     norm_blocks(blocks, normed_ref, vec(scale_ref), vec(shift_ref))
     normed = normed_ref[...]
     k_ref[...] = dot(normed, kw_ref[...]).astype(BF16)
     v_ref[...] = dot(normed, vw_ref[...]).astype(BF16)
-    halo = jnp.concatenate([normed_ref[:SIDE], normed_ref[TILE : TILE + TOP]], axis=0)
+    halo = jnp.concatenate([normed_ref[:SIDE], normed_ref[CUT : CUT + TOP]], axis=0)
     q_ref[...] = query(halo, qw_ref)
 
 
-def last_kernel(
-    mask_ref, cover_ref, pick_ref, tile_ref, east_ref, south_ref,
+def attend(q_ref, k_ref, v_ref, times, att_ref):
+    count = q_ref.shape[0]
+    shut = jnp.where(times > 0, 0.0, BLOCKED)
+    lane = lax.broadcasted_iota(jnp.int32, (count, LANES), 1)
+    ones = jnp.ones((KEYS, LANES), BF16)
+    for p in range(PAIRS):
+        at = slice(LANES * p, LANES * (p + 1))
+        q = q_ref[:, at]
+        zero = jnp.zeros_like(q)
+        both = jnp.concatenate([jnp.where(lane < HD, q, zero), jnp.where(lane < HD, zero, q)], axis=0)
+        scores = dot_t(both, k_ref[:, at]) + shut
+        top = jnp.max(scores, axis=-1, keepdims=True)
+        weights = (jnp.exp(scores - top) * times).astype(BF16)
+        out = dot(weights, jnp.concatenate([v_ref[:, at], ones], axis=1))
+        out = out[:, :LANES] / out[:, LANES:]
+        att_ref[:, at] = jnp.where(lane < HD, out[:count], out[count:]).astype(BF16)
+
+
+def live_times(mask_ref, cover_ref):
+    times = cover_ref[0:1]
+    for j in range(4):
+        times = times + cover_ref[j + 1 : j + 2] * (mask_ref[j] > 0).astype(F32)
+    return times
+
+
+def finish(tokens, att_ref, gate_ref, fscale_ref, fshift_ref, ow_ref, pw_ref, blend_ref, pick, spans):
+    count = tokens.shape[0]
+    mixed = tokens.astype(F32) + vec(gate_ref) * dot(att_ref[...], ow_ref[...])
+    final = layer_norm(mixed, vec(fscale_ref), vec(fshift_ref))
+    patch = dot_t(final, pw_ref[...])
+    spread = jnp.concatenate(
+        [jnp.broadcast_to(blend_ref[r : r + 1], (n, WW)) for r, n in spans], axis=0
+    )
+    b = jnp.sum(spread * pick, axis=1, keepdims=True)
+    return jnp.concatenate([b * patch, jnp.broadcast_to(b, (count, P_SIZE))], axis=1)
+
+
+def spill_kernel(
+    mask_ref, cover_ref, pick_ref, east_ref, south_ref,
     relay_ref, side_ref, rest_ref, corner_ref,
-    q0_ref, k0_ref, v0_ref, q1_ref, k1_ref, v1_ref,
+    k0_ref, v0_ref, q1_ref, k1_ref, v1_ref,
     scale_ref, shift_ref, gate_ref, fscale_ref, fshift_ref,
     qw_ref, kw_ref, vw_ref, ow_ref, pw_ref, blend_ref,
-    kept_ref, spill_e_ref, spill_s_ref, spill_c_ref,
-    normed_ref, queries_ref, keys_ref, vals_ref, att_ref,
+    spill_e_ref, spill_s_ref, spill_c_ref, keys_ref, vals_ref,
+    normed_ref, queries_ref, att_ref,
 ):
     norm_blocks((relay_ref, side_ref, rest_ref, corner_ref), normed_ref, vec(scale_ref), vec(shift_ref))
     normed = normed_ref[...]
-    queries_ref[:TILE] = q0_ref[...]
-    queries_ref[TILE : OWN - CORNER] = q1_ref[...]
-    queries_ref[OWN - CORNER :] = query(normed_ref[: 2 * CORNER], qw_ref)[:CORNER]
+    halo = SIDE + TOP
+    queries_ref[:halo] = q1_ref[...]
+    queries_ref[halo:] = query(normed_ref[: 2 * CORNER], qw_ref)[:CORNER]
     keys_ref[:TILE] = k0_ref[...]
     keys_ref[TILE:EARLY] = k1_ref[...]
     keys_ref[EARLY:] = dot(normed, kw_ref[...]).astype(BF16)
-    values = dot(normed, vw_ref[...]).astype(BF16)
-
-    times = cover_ref[0:1]
-    for j in range(4):
-        times = times + cover_ref[j + 1 : j + 2] * (mask_ref[j] > 0).astype(F32)
-    shut = jnp.where(times > 0, 0.0, BLOCKED)
-    lane = lax.broadcasted_iota(jnp.int32, (OWN, LANES), 1)
-    for p in range(PAIRS):
-        at = slice(LANES * p, LANES * (p + 1))
-        vals_ref[:TILE, :LANES] = v0_ref[:, at]
-        vals_ref[TILE:EARLY, :LANES] = v1_ref[:, at]
-        vals_ref[EARLY:, :LANES] = values[:, at]
-        if p == 0:
-            vals_ref[:, LANES:] = jnp.ones((KEYS, LANES), BF16)
-        q = queries_ref[:, at]
-        zero = jnp.zeros_like(q)
-        both = jnp.concatenate([jnp.where(lane < HD, q, zero), jnp.where(lane < HD, zero, q)], axis=0)
-        scores = dot_t(both, keys_ref[:, at]) + shut
-        top = jnp.max(scores, axis=-1, keepdims=True)
-        weights = (jnp.exp(scores - top) * times).astype(BF16)
-        out = dot(weights, vals_ref[...])
-        out = out[:, :LANES] / out[:, LANES:]
-        att_ref[:, at] = jnp.where(lane < HD, out[:OWN], out[OWN:]).astype(BF16)
-
-    window = jnp.concatenate(
-        [tile_ref[...], east_ref[:SIDE], south_ref[:TOP], relay_ref[:CORNER]], axis=0
-    )
-    mixed = window.astype(F32) + vec(gate_ref) * dot(att_ref[...], ow_ref[...])
-    final = layer_norm(mixed, vec(fscale_ref), vec(fshift_ref))
-    patch = dot_t(final, pw_ref[...])
-    spans = [(r, TW) for r in range(TH)] + [(r, EW) for r in range(TH)]
+    vals_ref[:TILE] = v0_ref[...]
+    vals_ref[TILE:EARLY] = v1_ref[...]
+    vals_ref[EARLY:] = dot(normed, vw_ref[...]).astype(BF16)
+    attend(queries_ref, keys_ref, vals_ref, live_times(mask_ref, cover_ref), att_ref)
+    tokens = jnp.concatenate([east_ref[:SIDE], south_ref[:TOP], relay_ref[:CORNER]], axis=0)
+    spans = [(r, EW) for r in range(TH)]
     spans += [(r, TW) for r in range(TH, WH)] + [(r, EW) for r in range(TH, WH)]
-    spread = jnp.concatenate(
-        [jnp.broadcast_to(blend_ref[r : r + 1], (n, WW)) for r, n in spans], axis=0
-    )
-    b = jnp.sum(spread * pick_ref[...], axis=1, keepdims=True)
-    both = jnp.concatenate([b * patch, jnp.broadcast_to(b, (OWN, P_SIZE))], axis=1)
-    kept_ref[...] = both[:TILE]
-    spill_e_ref[...] = both[TILE : TILE + SIDE]
-    spill_s_ref[...] = both[TILE + SIDE : OWN - CORNER]
-    spill_c_ref[...] = both[OWN - CORNER :]
+    both = finish(
+        tokens, att_ref, gate_ref, fscale_ref, fshift_ref, ow_ref, pw_ref, blend_ref,
+        pick_ref[TILE:], spans,
+    )
+    spill_e_ref[...] = both[:SIDE]
+    spill_s_ref[...] = both[SIDE:halo]
+    spill_c_ref[...] = both[halo:]
+
+
+def kept_kernel(
+    mask_ref, cover_ref, pick_ref, tile_ref, q_ref, keys_ref, vals_ref,
+    gate_ref, fscale_ref, fshift_ref, ow_ref, pw_ref, blend_ref,
+    kept_ref,
+    att_ref,
+):
+    attend(q_ref, keys_ref, vals_ref, live_times(mask_ref, cover_ref), att_ref)
+    kept_ref[...] = finish(
+        tile_ref[...], att_ref, gate_ref, fscale_ref, fshift_ref, ow_ref, pw_ref, blend_ref,
+        pick_ref[:TILE], [(r, TW) for r in range(TH)],
+    )
 
 
 def blend_kernel(kept_ref, left_ref, upper_ref, corner_ref, out_ref):
@@ -277,14 +304,15 @@
     blend_weight,
 ):
     mask = neighbour_mask.reshape(4)
-    tile, top, rest, packed, side = call(
+    tile, top, rest, near, body, side = call(
         pack_kernel,
-        [((n, D), BF16) for n in (TILE, TOP, REST, TILE, SIDE)],
+        [((n, D), BF16) for n in (TILE, TOP, REST, CUT, TILE - CUT, SIDE)],
         latent,
         limit=4 * MB,
         flops=1 << 33,
     )
-    east, far = fetch(packed, 0, 1), fetch(side, 0, 2)
+    east, far = fetch(near, 0, 1), fetch(side, 0, 2)
+    east_body = fetch(body, 0, 1)
     west_top, west_rest = fetch(top, 0, -1), fetch(rest, 0, -1)
     north, south = fetch(tile, -1, 0), fetch(tile, 1, 0)
     low = fetch(top, 2, 0)
@@ -306,32 +334,36 @@
     q1, k1, v1 = call(
         mid_kernel,
         [((n, AD), BF16) for n in (SIDE + TOP, EARLY - TILE, EARLY - TILE)],
-        east, south, far, north, low, west_top,
+        east, south, far, north, low, west_top, east_body,
         attn_scale, attn_shift, q_weight, k_weight, v_weight,
         scratch=[((EARLY - TILE, D), BF16)],
         limit=12 * MB,
     )
-    kept, spill_e, spill_s, spill_c = call(
-        last_kernel,
-        [((n, LANES), F32) for n in (TILE, SIDE, TOP, CORNER)],
-        mask, jnp.asarray(coverage()), jnp.asarray(query_columns()), tile, east, south,
+    cover, pick, out_t = jnp.asarray(coverage()), jnp.asarray(query_columns()), out_weight.T
+    spill_e, spill_s, spill_c, keys, vals = call(
+        spill_kernel,
+        [((n, LANES), F32) for n in (SIDE, TOP, CORNER)] + [((KEYS, AD), BF16)] * 2,
+        mask, cover, pick, east, south,
         relayed, north_side, west_rest, low_corner,
-        q0, k0, v0, q1, k1, v1,
+        k0, v0, q1, k1, v1,
         attn_scale, attn_shift, attn_gate, final_scale, final_shift,
-        q_weight, k_weight, v_weight, o_weight, out_weight.T, blend_weight,
-        scratch=[
-            ((LATE, D), BF16),
-            ((OWN, AD), BF16),
-            ((KEYS, AD), BF16),
-            ((KEYS, 2 * LANES), BF16),
-            ((OWN, AD), BF16),
-        ],
+        q_weight, k_weight, v_weight, o_weight, out_t, blend_weight,
+        scratch=[((LATE, D), BF16), ((OWN - TILE, AD), BF16), ((OWN - TILE, AD), BF16)],
         smem=1,
-        limit=20 * MB,
+        limit=16 * MB,
     )
     left = fetch(spill_e, 0, -1)
     diag = fetch(spill_c, -1, -1)
     upper = fetch(spill_s, -1, 0)
+    (kept,) = call(
+        kept_kernel,
+        [((TILE, LANES), F32)],
+        mask, cover, pick, tile, q0, keys, vals,
+        attn_gate, final_scale, final_shift, o_weight, out_t, blend_weight,
+        scratch=[((TILE, AD), BF16)],
+        smem=1,
+        limit=16 * MB,
+    )
     (out,) = call(blend_kernel, [((TH, TW * P_SIZE), F32)], kept, left, upper, diag, limit=4 * MB)
     return out
 

time: 42.1 us -> 37.7 us (0.90)
  waiting for transfers between devices: 17.4 us -> 11.5 us
  Pallas kernels: 9.2 us -> 10.7 us
    ppermute x13 -> x14, waiting for transfers between devices: 17.4 us -> 11.5 us  [fetch(): return lax.ppermute(block, ('row', 'col'), route)]
    pallas_call x6 -> x7, Pallas kernels: 9.2 us -> 10.7 us  [call(): pl.pallas_call(kernel, out_shape=[jax.ShapeDtypeStruct(s, d) for s, d in...]
    ppermute x13 -> x14, starting transfers between devices: 13.9 us -> 13.8 us  [fetch(): return lax.ppermute(block, ('row', 'col'), route)]
  transfers between devices with their start and end apart: 13 -> 14, of which waited for: 3 -> 4; matrix products, arithmetic and copies ran while one was open for 0% -> 0% of each run, Pallas kernels for 9% -> 16%
where the time goes in v4:
time: 37.7 us; the launch traced here: 37.5 us
  starting transfers between devices  13.8 us (37%)
  waiting for transfers between devices  11.5 us (31%)
  Pallas kernels  10.7 us (28%)
  local copies, waits for them, and re-layouts  1.18 us (3%)
    ppermute x14, starting transfers between devices, fetch(): return lax.ppermute(block, ('row', 'col'), route)  13.8 us
    ppermute x14, waiting for transfers between devices, fetch(): return lax.ppermute(block, ('row', 'col'), route)  11.5 us
    pallas_call x7, Pallas kernels, call(): pl.pallas_call(kernel, out_shape=[jax.ShapeDtypeStruct(s, d) for s, d in...  10.7 us
    unnamed x30, local copies, waits for them, and re-layouts  1.18 us
  transfers between devices with their start and end apart: 14, of which 4 were waited for; matrix products, arithmetic and copies ran while one was open for 0% of the time, Pallas kernels for 16%

profile of v4, /device:TPU:0, one launch (start us, length us, event | category | flops | bytes accessed | tf_op | source)
XLA Modules:
  0.0 37.5 jit_solution(5630247374350100073)
XLA Ops:
  0.0 1.1 %copy-done.14 = bf16[6,12,1536]{2,1,0:T(8,128)(2,1)S(1)} copy-done((bf16[6,12,1536]{2,1,0:T(8,128)(2,1)S(1)}, bf16[6,12,1536]{2,1,0:T(8,128)(2,1)}, u32[]{:S(2)}) %copy-start.14) | copy-done | bytes 221208
  1.1 0.1 shard_map.145
  1.2 6.1 %collective-permute-start = (bf16[40,1536]{1,0:T(8,128)(2,1)S(1)}, bf16[40,1536]{1,0:T(8,128)(2,1)S(1)}, u32[]{:S(2)}, u32[]{:S(2)}) collective-permute-start(bf16[40,1536]{1,0:T(8,128)(2,1)S(1)} %get-tuple-element.27), channel_id=1, source_target_pairs={{1,0},{2,1},{3,2},{4,3},{5,4},{6,5},{7,6},{0,7},{9,8},{10,9},{11,1... | collective-permute-start | bytes 368648 | tf_op jit(solution)/shard_map/ppermute | solution.py:97
  7.3 0.4 %collective-permute-start.2 = (bf16[24,1536]{1,0:T(8,128)(2,1)S(1)}, bf16[24,1536]{1,0:T(8,128)(2,1)S(1)}, u32[]{:S(2)}, u32[]{:S(2)}) collective-permute-start(bf16[24,1536]{1,0:T(8,128)(2,1)S(1)} %get-tuple-element.28), channel_id=1, source_target_pairs={{2,0},{3,1},{4,2},{5,3},{6,4},{7,5},{0,6},{1,7},{10,8},{11,9},{12,... | collective-permute-start | bytes 221192 | tf_op jit(solution)/shard_map/ppermute | solution.py:97
  7.8 0.6 %collective-permute-start.3 = (bf16[24,1536]{1,0:T(8,128)(2,1)S(1)}, bf16[24,1536]{1,0:T(8,128)(2,1)S(1)}, u32[]{:S(2)}, u32[]{:S(2)}) collective-permute-start(bf16[24,1536]{1,0:T(8,128)(2,1)S(1)} %get-tuple-element.29), channel_id=1, source_target_pairs={{7,0},{0,1},{1,2},{2,3},{3,4},{4,5},{5,6},{6,7},{15,8},{8,9},{9,10... | collective-permute-start | bytes 221192 | tf_op jit(solution)/shard_map/ppermute | solution.py:97
  8.4 1.5 %collective-permute-start.9 = (bf16[24,1536]{1,0:T(8,128)(2,1)S(1)}, bf16[24,1536]{1,0:T(8,128)(2,1)S(1)}, u32[]{:S(2)}, u32[]{:S(2)}) collective-permute-start(bf16[24,1536]{1,0:T(8,128)(2,1)S(1)} %get-tuple-element.29), channel_id=1, source_target_pairs={{16,0},{17,1},{18,2},{19,3},{20,4},{21,5},{22,6},{23,7},{24,8},{25... | collective-permute-start | bytes 221192 | tf_op jit(solution)/shard_map/ppermute | solution.py:97
  9.9 1.8 %collective-permute-done.2.far_ref = bf16[24,1536]{1,0:T(8,128)(2,1)S(1)} collective-permute-done((bf16[24,1536]{1,0:T(8,128)(2,1)S(1)}, bf16[24,1536]{1,0:T(8,128)(2,1)S(1)}, u32[]{:S(2)}, u32[]{:S(2)}) %collective-permute-start.2) | collective-permute-done | bytes 73760 | tf_op jit(solution)/shard_map/ppermute | solution.py:97
  11.7 3.1 %collective-permute-done.3.top_ref.west_ref = bf16[24,1536]{1,0:T(8,128)(2,1)S(1)} collective-permute-done((bf16[24,1536]{1,0:T(8,128)(2,1)S(1)}, bf16[24,1536]{1,0:T(8,128)(2,1)S(1)}, u32[]{:S(2)}, u32[]{:S(2)}) %collective-permute-start.3) | collective-permute-done | bytes 73760 | tf_op jit(solution)/shard_map/ppermute | solution.py:97
  14.8 0.1 collective-permute-start.4
  14.9 1.1 %collective-permute-start.10 = (bf16[32,1536]{1,0:T(8,128)(2,1)S(1)}, bf16[32,1536]{1,0:T(8,128)(2,1)S(1)}, u32[]{:S(2)}, u32[]{:S(2)}) collective-permute-start(bf16[32,1536]{1,0:T(8,128)(2,1)S(1)} %get-tuple-element.36), channel_id=1, source_target_pairs={{1,0},{2,1},{3,2},{4,3},{5,4},{6,5},{7,6},{0,7},{9,8},{10,9},{11,1... | collective-permute-start | bytes 294920 | tf_op jit(solution)/shard_map/ppermute | solution.py:97
  16.0 0.9 %collective-permute-start.6 = (bf16[48,1536]{1,0:T(8,128)(2,1)S(1)}, bf16[48,1536]{1,0:T(8,128)(2,1)S(1)}, u32[]{:S(2)}, u32[]{:S(2)}) collective-permute-start(bf16[48,1536]{1,0:T(8,128)(2,1)S(1)} %get-tuple-element.32), channel_id=1, source_target_pairs={{7,0},{0,1},{1,2},{2,3},{3,4},{4,5},{5,6},{6,7},{15,8},{8,9},{9,10... | collective-permute-start | bytes 442376 | tf_op jit(solution)/shard_map/ppermute | solution.py:97
  17.0 3.1 %collective-permute-done.10.body_ref = bf16[32,1536]{1,0:T(8,128)(2,1)S(1)} collective-permute-done((bf16[32,1536]{1,0:T(8,128)(2,1)S(1)}, bf16[32,1536]{1,0:T(8,128)(2,1)S(1)}, u32[]{:S(2)}, u32[]{:S(2)}) %collective-permute-start.10) | collective-permute-done | bytes 98336 | tf_op jit(solution)/shard_map/ppermute | solution.py:97
  20.1 1.5 %collective-permute-start.7 = (bf16[8,1536]{1,0:T(8,128)(2,1)S(1)}, bf16[8,1536]{1,0:T(8,128)(2,1)S(1)}, u32[]{:S(2)}, u32[]{:S(2)}) collective-permute-start(bf16[8,1536]{1,0:T(8,128)(2,1)S(1)} %get-tuple-element.33), channel_id=1, source_target_pairs={{16,0},{17,1},{18,2},{19,3},{20,4},{21,5},{22,6},{23,7},{24,8},{25... | collective-permute-start | bytes 73736 | tf_op jit(solution)/shard_map/ppermute | solution.py:97
  21.6 1.5 %shard_map.146 = (bf16[72,768]{1,0:T(8,128)(2,1)S(1)}, bf16[72,768]{1,0:T(8,128)(2,1)S(1)}, bf16[72,768]{1,0:T(8,128)(2,1)S(1)}) custom-call(bf16[72,1536]{1,0:T(8,128)(2,1)S(1)} %get-tuple-element.25.tile_ref, f32[1536]{0:T(1024)S(1)} %copy-done.6, f32[1536]{0:T(1024)S(1)} %copy-done.7, bf16[1536,768]{1,0:T(8,128)(2,1)S(1)} %copy-done, ...), custom_call_target="tpu_custom_call" | custom-call | tf_op jit(solution)/shard_map/pallas_call | solution.py:280
  23.2 0.0 copy-start.5
  23.2 0.0 copy-start.8
  23.3 2.3 %shard_map.148 = (bf16[48,768]{1,0:T(8,128)(2,1)S(1)}, bf16[288,768]{1,0:T(8,128)(2,1)S(1)}, bf16[288,768]{1,0:T(8,128)(2,1)S(1)}) custom-call(bf16[40,1536]{1,0:T(8,128)(2,1)S(1)} %collective-permute-done.east_ref, bf16[72,1536]{1,0:T(8,128)(2,1)S(1)} %collective-permute-done.1.south_ref, bf16[24,1536]{1,0:T(8,128)(2,1)S(1)} %collective-permute-done.2.far_ref, ...), custom_call_target="tpu_custom_call" | custom-call | tf_op jit(solution)/shard_map/pallas_call | solution.py:280
  25.8 3.7 %shard_map.149 = (f32[24,128]{1,0:T(8,128)S(1)}, f32[24,128]{1,0:T(8,128)S(1)}, f32[8,128]{1,0:T(8,128)S(1)}, bf16[512,768]{1,0:T(8,128)(2,1)S(1)}, bf16[512,768]{1,0:T(8,128)(2,1)S(1)}) custom-call(s32[4]{0:T(128)S(1)} %bitcast.4, f32[8,512]{1,0:T(8,128)S(1)} %copy-done.8, f32[128,16]{1,0:T(8,128)S(1)} %copy-done.5, ...), custom_call_target="tpu_custom_call" | custom-call | tf_op jit(solution)/shard_map/pallas_call | solution.py:280
  29.5 0.1 collective-permute-start.11
  29.5 0.4 %collective-permute-start.12 = (f32[24,128]{1,0:T(8,128)S(1)}, f32[24,128]{1,0:T(8,128)S(1)}, u32[]{:S(2)}, u32[]{:S(2)}) collective-permute-start(f32[24,128]{1,0:T(8,128)S(1)} %get-tuple-element.43), channel_id=1, source_target_pairs={{24,0},{25,1},{26,2},{27,3},{28,4},{29,5},{30,6},{31,7},{0,8},{1,9... | collective-permute-start | bytes 36872 | tf_op jit(solution)/shard_map/ppermute | solution.py:97
  29.9 1.1 %collective-permute-start.13 = (f32[8,128]{1,0:T(8,128)S(1)}, f32[8,128]{1,0:T(8,128)S(1)}, u32[]{:S(2)}, u32[]{:S(2)}) collective-permute-start(f32[8,128]{1,0:T(8,128)S(1)} %get-tuple-element.44), channel_id=1, source_target_pairs={{31,0},{24,1},{25,2},{26,3},{27,4},{28,5},{29,6},{30,7},{7,8},{0,9... | collective-permute-start | bytes 12296 | tf_op jit(solution)/shard_map/ppermute | solution.py:97
  31.0 2.3 %shard_map.150.kept_ref = f32[72,128]{1,0:T(8,128)S(1)} custom-call(s32[4]{0:T(128)S(1)} %bitcast.5, f32[8,512]{1,0:T(8,128)S(1)} %copy-done.8, f32[128,16]{1,0:T(8,128)S(1)} %copy-done.5, bf16[72,1536]{1,0:T(8,128)(2,1)S(1)} %get-tuple-element.25.tile_ref, bf16[72,768]{1,0:T(8,128)(2,1)S(1)} %get-tuple-element.26.q_ref, ...), custom_call_target="tpu_custom_call" | custom-call | tf_op jit(solution)/shard_map/pallas_call | solution.py:280
  33.3 3.4 %collective-permute-done.13.corner_ref = f32[8,128]{1,0:T(8,128)S(1)} collective-permute-done((f32[8,128]{1,0:T(8,128)S(1)}, f32[8,128]{1,0:T(8,128)S(1)}, u32[]{:S(2)}, u32[]{:S(2)}) %collective-permute-start.13) | collective-permute-done | bytes 4128 | tf_op jit(solution)/shard_map/ppermute | solution.py:97
  36.7 0.8 %shard_map.151 = f32[6,768]{1,0:T(8,128)} custom-call(f32[72,128]{1,0:T(8,128)S(1)} %shard_map.150.kept_ref, f32[24,128]{1,0:T(8,128)S(1)} %collective-permute-done.11.left_ref, f32[24,128]{1,0:T(8,128)S(1)} %collective-permute-done.12.upper_ref, f32[8,128]{1,0:T(8,128)S(1)} %collective-permute-done.13.corner_ref), custom_call_target="tpu_custom_call" | custom-call | tf_op jit(solution)/shard_map/pallas_call | solution.py:280
  (41 shorter events, 0.1 us)
Async XLA Ops:
  0.0 21.6 %copy-start.2 = (bf16[1536,768]{1,0:T(8,128)(2,1)S(1)}, bf16[1536,768]{1,0:T(8,128)(2,1)}, u32[]{:S(2)}) copy-start(bf16[1536,768]{1,0:T(8,128)(2,1)} %vw_ref.5) | copy-start | bytes 7077892
  0.0 21.6 %copy-start.1 = (bf16[1536,768]{1,0:T(8,128)(2,1)S(1)}, bf16[1536,768]{1,0:T(8,128)(2,1)}, u32[]{:S(2)}) copy-start(bf16[1536,768]{1,0:T(8,128)(2,1)} %kw_ref.5) | copy-start | bytes 7077892
  0.0 21.6 %copy-start = (bf16[1536,768]{1,0:T(8,128)(2,1)S(1)}, bf16[1536,768]{1,0:T(8,128)(2,1)}, u32[]{:S(2)}) copy-start(bf16[1536,768]{1,0:T(8,128)(2,1)} %qw_ref.5) | copy-start | bytes 7077892
  0.0 21.6 %copy-start.6 = (f32[1536]{0:T(1024)S(1)}, f32[1536]{0:T(1024)}, u32[]{:S(2)}) copy-start(f32[1536]{0:T(1024)} %scale_ref.5) | copy-start | bytes 18436
  0.0 21.6 %copy-start.7 = (f32[1536]{0:T(1024)S(1)}, f32[1536]{0:T(1024)}, u32[]{:S(2)}) copy-start(f32[1536]{0:T(1024)} %shift_ref.5) | copy-start | bytes 18436
  1.2 13.6 %collective-permute-start = (bf16[40,1536]{1,0:T(8,128)(2,1)S(1)}, bf16[40,1536]{1,0:T(8,128)(2,1)S(1)}, u32[]{:S(2)}, u32[]{:S(2)}) collective-permute-start(bf16[40,1536]{1,0:T(8,128)(2,1)S(1)} %get-tuple-element.27), channel_id=1, source_target_pairs={{1,0},{2,1},{3,2},{4,3},{5,4},{6,5},{7,6},{0,7},{9,8},{10,9},{11,1... | collective-permute-start | bytes 368648 | tf_op jit(solution)/shard_map/ppermute | solution.py:97
  7.3 4.4 %collective-permute-start.2 = (bf16[24,1536]{1,0:T(8,128)(2,1)S(1)}, bf16[24,1536]{1,0:T(8,128)(2,1)S(1)}, u32[]{:S(2)}, u32[]{:S(2)}) collective-permute-start(bf16[24,1536]{1,0:T(8,128)(2,1)S(1)} %get-tuple-element.28), channel_id=1, source_target_pairs={{2,0},{3,1},{4,2},{5,3},{6,4},{7,5},{0,6},{1,7},{10,8},{11,9},{12,... | collective-permute-start | bytes 221192 | tf_op jit(solution)/shard_map/ppermute | solution.py:97
  7.8 7.0 %collective-permute-start.3 = (bf16[24,1536]{1,0:T(8,128)(2,1)S(1)}, bf16[24,1536]{1,0:T(8,128)(2,1)S(1)}, u32[]{:S(2)}, u32[]{:S(2)}) collective-permute-start(bf16[24,1536]{1,0:T(8,128)(2,1)S(1)} %get-tuple-element.29), channel_id=1, source_target_pairs={{7,0},{0,1},{1,2},{2,3},{3,4},{4,5},{5,6},{6,7},{15,8},{8,9},{9,10... | collective-permute-start | bytes 221192 | tf_op jit(solution)/shard_map/ppermute | solution.py:97
  8.4 11.7 %collective-permute-start.8 = (bf16[72,1536]{1,0:T(8,128)(2,1)S(1)}, bf16[72,1536]{1,0:T(8,128)(2,1)S(1)}, u32[]{:S(2)}, u32[]{:S(2)}) collective-permute-start(bf16[72,1536]{1,0:T(8,128)(2,1)S(1)} %get-tuple-element.25.tile_ref), channel_id=1, source_target_pairs={{24,0},{25,1},{26,2},{27,3},{28,4},{29,5},{30,6},{31,7},{0,8},{1,9... | collective-permute-start | bytes 663560 | tf_op jit(solution)/shard_map/ppermute | solution.py:97
  8.4 7.7 %collective-permute-start.9 = (bf16[24,1536]{1,0:T(8,128)(2,1)S(1)}, bf16[24,1536]{1,0:T(8,128)(2,1)S(1)}, u32[]{:S(2)}, u32[]{:S(2)}) collective-permute-start(bf16[24,1536]{1,0:T(8,128)(2,1)S(1)} %get-tuple-element.29), channel_id=1, source_target_pairs={{16,0},{17,1},{18,2},{19,3},{20,4},{21,5},{22,6},{23,7},{24,8},{25... | collective-permute-start | bytes 221192 | tf_op jit(solution)/shard_map/ppermute | solution.py:97
  11.7 11.6 %collective-permute-start.1 = (bf16[72,1536]{1,0:T(8,128)(2,1)S(1)}, bf16[72,1536]{1,0:T(8,128)(2,1)S(1)}, u32[]{:S(2)}, u32[]{:S(2)}) collective-permute-start(bf16[72,1536]{1,0:T(8,128)(2,1)S(1)} %get-tuple-element.25.tile_ref), channel_id=1, source_target_pairs={{8,0},{9,1},{10,2},{11,3},{12,4},{13,5},{14,6},{15,7},{16,8},{17,9... | collective-permute-start | bytes 663560 | tf_op jit(solution)/shard_map/ppermute | solution.py:97
  14.8 10.8 %collective-permute-start.4 = (bf16[72,1536]{1,0:T(8,128)(2,1)S(1)}, bf16[72,1536]{1,0:T(8,128)(2,1)S(1)}, u32[]{:S(2)}, u32[]{:S(2)}) collective-permute-start(bf16[72,1536]{1,0:T(8,128)(2,1)S(1)} %get-tuple-element.30), channel_id=1, source_target_pairs={{8,0},{9,1},{10,2},{11,3},{12,4},{13,5},{14,6},{15,7},{16,8},{17,9... | collective-permute-start | bytes 663560 | tf_op jit(solution)/shard_map/ppermute | solution.py:97
  14.9 5.2 %collective-permute-start.10 = (bf16[32,1536]{1,0:T(8,128)(2,1)S(1)}, bf16[32,1536]{1,0:T(8,128)(2,1)S(1)}, u32[]{:S(2)}, u32[]{:S(2)}) collective-permute-start(bf16[32,1536]{1,0:T(8,128)(2,1)S(1)} %get-tuple-element.36), channel_id=1, source_target_pairs={{1,0},{2,1},{3,2},{4,3},{5,4},{6,5},{7,6},{0,7},{9,8},{10,9},{11,1... | collective-permute-start | bytes 294920 | tf_op jit(solution)/shard_map/ppermute | solution.py:97
  16.0 9.6 %collective-permute-start.6 = (bf16[48,1536]{1,0:T(8,128)(2,1)S(1)}, bf16[48,1536]{1,0:T(8,128)(2,1)S(1)}, u32[]{:S(2)}, u32[]{:S(2)}) collective-permute-start(bf16[48,1536]{1,0:T(8,128)(2,1)S(1)} %get-tuple-element.32), channel_id=1, source_target_pairs={{7,0},{0,1},{1,2},{2,3},{3,4},{4,5},{5,6},{6,7},{15,8},{8,9},{9,10... | collective-permute-start | bytes 442376 | tf_op jit(solution)/shard_map/ppermute | solution.py:97
  20.1 5.6 %collective-permute-start.5 = (bf16[24,1536]{1,0:T(8,128)(2,1)S(1)}, bf16[24,1536]{1,0:T(8,128)(2,1)S(1)}, u32[]{:S(2)}, u32[]{:S(2)}) collective-permute-start(bf16[24,1536]{1,0:T(8,128)(2,1)S(1)} %get-tuple-element.31), channel_id=1, source_target_pairs={{24,0},{25,1},{26,2},{27,3},{28,4},{29,5},{30,6},{31,7},{0,8},{1,9... | collective-permute-start | bytes 221192 | tf_op jit(solution)/shard_map/ppermute | solution.py:97
  20.1 5.6 %collective-permute-start.7 = (bf16[8,1536]{1,0:T(8,128)(2,1)S(1)}, bf16[8,1536]{1,0:T(8,128)(2,1)S(1)}, u32[]{:S(2)}, u32[]{:S(2)}) collective-permute-start(bf16[8,1536]{1,0:T(8,128)(2,1)S(1)} %get-tuple-element.33), channel_id=1, source_target_pairs={{16,0},{17,1},{18,2},{19,3},{20,4},{21,5},{22,6},{23,7},{24,8},{25... | collective-permute-start | bytes 73736 | tf_op jit(solution)/shard_map/ppermute | solution.py:97
  23.2 2.5 %copy-start.3 = (bf16[768,1536]{1,0:T(8,128)(2,1)S(1)}, bf16[768,1536]{1,0:T(8,128)(2,1)}, u32[]{:S(2)}) copy-start(bf16[768,1536]{1,0:T(8,128)(2,1)} %ow_ref.3) | copy-start | bytes 7077892
  23.2 2.5 %copy-start.4 = (bf16[1536,64]{0,1:T(8,128)(2,1)S(1)}, bf16[1536,64]{0,1:T(8,128)(2,1)}, u32[]{:S(2)}) copy-start(bf16[1536,64]{0,1:T(8,128)(2,1)} %param.25) | copy-start | bytes 589828
  23.2 2.5 %copy-start.5 = (f32[128,16]{1,0:T(8,128)S(1)}, f32[128,16]{1,0:T(8,128)}, u32[]{:S(2)}) copy-start(f32[128,16]{1,0:T(8,128)} %constant.5.clone.pick_ref) | copy-start | bytes 24580
  23.2 2.5 %copy-start.8 = (f32[8,512]{1,0:T(8,128)S(1)}, f32[8,512]{1,0:T(8,128)}, u32[]{:S(2)}) copy-start(f32[8,512]{1,0:T(8,128)} %constant.4.clone.cover_ref) | copy-start | bytes 49156
  23.2 2.5 %copy-start.9 = (f32[1536]{0:T(1024)S(1)}, f32[1536]{0:T(1024)}, u32[]{:S(2)}) copy-start(f32[1536]{0:T(1024)} %gate_ref.3) | copy-start | bytes 18436
  29.5 7.3 %collective-permute-start.11 = (f32[24,128]{1,0:T(8,128)S(1)}, f32[24,128]{1,0:T(8,128)S(1)}, u32[]{:S(2)}, u32[]{:S(2)}) collective-permute-start(f32[24,128]{1,0:T(8,128)S(1)} %get-tuple-element.42), channel_id=1, source_target_pairs={{7,0},{0,1},{1,2},{2,3},{3,4},{4,5},{5,6},{6,7},{15,8},{8,9},{9,10... | collective-permute-start | bytes 36872 | tf_op jit(solution)/shard_map/ppermute | solution.py:97
  29.5 7.2 %collective-permute-start.12 = (f32[24,128]{1,0:T(8,128)S(1)}, f32[24,128]{1,0:T(8,128)S(1)}, u32[]{:S(2)}, u32[]{:S(2)}) collective-permute-start(f32[24,128]{1,0:T(8,128)S(1)} %get-tuple-element.43), channel_id=1, source_target_pairs={{24,0},{25,1},{26,2},{27,3},{28,4},{29,5},{30,6},{31,7},{0,8},{1,9... | collective-permute-start | bytes 36872 | tf_op jit(solution)/shard_map/ppermute | solution.py:97
  29.9 6.8 %collective-permute-start.13 = (f32[8,128]{1,0:T(8,128)S(1)}, f32[8,128]{1,0:T(8,128)S(1)}, u32[]{:S(2)}, u32[]{:S(2)}) collective-permute-start(f32[8,128]{1,0:T(8,128)S(1)} %get-tuple-element.44), channel_id=1, source_target_pairs={{31,0},{24,1},{25,2},{26,3},{27,4},{28,5},{29,6},{30,7},{7,8},{0,9... | collective-permute-start | bytes 12296 | tf_op jit(solution)/shard_map/ppermute | solution.py:97
  (5 other events, 11.1 us)
